TPU v7x, 256 devices: a whole 4x4x8 slice. The times are simulated.
256 devices in a mesh: gx: 4 (over x), gy: 8 (over z_hi, y), gz: 8 (over z_lo, core).
Axes of the slice: x: 4, y: 4, z: 8 (z_hi: 2, z_lo: 4; z = z_hi * 4 + z_lo), core: 2. Of those that a mesh axis runs over, the one named last changes fastest.
Arguments:
- velocity: float32 [3, 128, 768, 2048], P(None, 'gx', 'gy', 'gz'), may hold values from -6 to 6
Outputs:
- magnitude: float32 [128, 768, 2048], P('gx', ('gy', 'gz'))
- level_one: float32 [64, 384, 1024], P('gx', 'gy')
- level_two: float32 [32, 192, 512], P('gx', 'gy')
- level_three: float32 [16, 96, 256], P('gx', 'gy')
- level_four: float32 [8, 48, 128], P('gx', 'gy')
- level_five: float32 [4, 24, 64], P('gx', 'gy')
All inputs are finite; a program needn't handle non-finite values.
Results may differ from a plain program's by a relative error of at most 0.000075.
Values sent between devices are 32-bit elements; how exact they have to be, the bound alone decides.
No kernel may reach another device: no remote copies, remote signals or barrier semaphores. Data moves between devices by JAX's collectives and lax.ppermute only.
A program may use at most 256 MiB of HBM per device.

v0:
```python
import functools

import jax
import jax.numpy as jnp
from jax import lax
from jax.experimental import pallas as pl
from jax.experimental.pallas import tpu as pltpu
from jax.sharding import PartitionSpec as P


PLANES = 8
HIGHEST = lax.Precision.HIGHEST
F32 = jnp.float32


def pairing(depth):
    row = lax.broadcasted_iota(jnp.int32, (depth, depth // 2), 0)
    col = lax.broadcasted_iota(jnp.int32, (depth, depth // 2), 1)
    return (lax.div(row, jnp.int32(2)) == col).astype(F32)


def pair_lanes(value):
    _, depth = value.shape
    width = min(depth, 256)
    matrix = pairing(width)
    parts = [
        jnp.dot(value[:, i : i + width], matrix, precision=HIGHEST, preferred_element_type=F32)
        for i in range(0, depth, width)
    ]
    return parts[0] if len(parts) == 1 else jnp.concatenate(parts, axis=1)


def keep_rows(scratch, at, value):
    for t in range(scratch.shape[0]):
        scratch[t, at : at + value.shape[0], :] = value[:, t * 128 : (t + 1) * 128]


def pair_rows(scratch, pairs):
    parts = [
        scratch[t, pl.ds(0, pairs, stride=2), :] + scratch[t, pl.ds(1, pairs, stride=2), :]
        for t in range(scratch.shape[0])
    ]
    return parts[0] if len(parts) == 1 else jnp.concatenate(parts, axis=1)


def ends_kernel(vel, top, bottom, row_first, row_last, lane_first, lane_last):
    step = pl.program_id(0)
    _, planes, rows, depth = vel.shape
    lane = lax.broadcasted_iota(jnp.int32, (rows, 128), 1)
    first = lane_first[...]
    last = lane_last[...]
    for k in range(2):
        for p in range(planes):
            at = k * 32 + step * planes + p
            first = jnp.where(lane == at, pltpu.roll(vel[k, p, :, :128], at, 1), first)
            last = jnp.where(
                lane == at, pltpu.roll(vel[k, p, :, depth - 128 :], lax.rem(at + 1, 128), 1), last
            )
    lane_first[...] = first
    lane_last[...] = last
    for k, comp in enumerate((0, 2)):
        for p in range(planes):
            row_first[k, p : p + 1, :] = top[comp, p, 0:1, :]
            row_last[k, p : p + 1, :] = bottom[comp, p, 7:8, :]


def ends(velocity):
    _, X, Y, Z = velocity.shape
    rows = jax.ShapeDtypeStruct((2, X, Z), F32)
    lanes = jax.ShapeDtypeStruct((Y, 128), F32)
    return pl.pallas_call(
        ends_kernel,
        grid=(X // PLANES,),
        in_specs=[
            pl.BlockSpec((2, PLANES, Y, Z), lambda i: (0, i, 0, 0)),
            pl.BlockSpec((3, PLANES, 8, Z), lambda i: (0, i, 0, 0)),
            pl.BlockSpec((3, PLANES, 8, Z), lambda i: (0, i, Y // 8 - 1, 0)),
        ],
        out_specs=[
            pl.BlockSpec((2, PLANES, Z), lambda i: (0, i, 0)),
            pl.BlockSpec((2, PLANES, Z), lambda i: (0, i, 0)),
            pl.BlockSpec((Y, 128), lambda i: (0, 0)),
            pl.BlockSpec((Y, 128), lambda i: (0, 0)),
        ],
        out_shape=[rows, rows, lanes, lanes],
        cost_estimate=pl.CostEstimate(flops=4_000_000, bytes_accessed=8_000_000, transcendentals=0),
        name="ends",
    )(velocity, velocity, velocity)


def curl_kernel(shifts, pos, vel, v_before, v_after, w_before, w_after, inner, *refs):
    x_before, x_after, y_before, y_after, z_before, z_after = refs[:6]
    mags = refs[-2 - len(shifts) - 1 : -3]
    level_out, summed, turned = refs[-3:]
    half, me = pos[0], pos[1]
    step = pl.program_id(0)
    _, planes, rows, depth = vel.shape
    each = rows // 4
    tall = 2 * each
    tiles = depth // 128
    lane = lax.broadcasted_iota(jnp.int32, (tall, depth), 1)
    at_first, at_last = lane == 0, lane == depth - 1
    lower = half == 0
    at_start = step == 0
    at_end = step == pl.num_programs(0) - 1

    for pair in range(planes // 2):
        for q in range(rows // tall):
            lo, hi = q * tall, (q + 1) * tall
            band = slice(lo, hi)
            both = []
            for p in (2 * pair, 2 * pair + 1):

                def first_diff(k):
                    if p + 1 < planes:
                        ahead = vel[k, p + 1, band, :]
                    else:
                        near = (v_after, w_after)[k - 1][0, 0, band, :]
                        ahead = jnp.where(at_end, x_after[k - 1, band, :], near)
                    if p > 0:
                        behind = vel[k, p - 1, band, :]
                    else:
                        near = (v_before, w_before)[k - 1][0, 0, band, :]
                        behind = jnp.where(at_start, x_before[k - 1, band, :], near)
                    return ahead - behind

                def second_diff(k):
                    slot = 0 if k == 0 else 1
                    if lo == 0:
                        edge = jnp.where(lower, y_before[slot, p : p + 1, :], inner[k, p, 7:8, :])
                        behind = jnp.concatenate([edge, vel[k, p, 0 : hi - 1, :]], axis=0)
                    else:
                        behind = vel[k, p, lo - 1 : hi - 1, :]
                    if hi == rows:
                        edge = jnp.where(lower, inner[k, p, 0:1, :], y_after[slot, p : p + 1, :])
                        ahead = jnp.concatenate([vel[k, p, lo + 1 : hi, :], edge], axis=0)
                    else:
                        ahead = vel[k, p, lo + 1 : hi + 1, :]
                    return ahead - behind

                def third_diff(k):
                    field = vel[k, p, band, :]
                    at = k * 32 + step * planes + p
                    fill = jnp.concatenate(
                        [
                            pltpu.roll(z_before[band, :], lax.rem(128 - at, 128), 1),
                            pltpu.roll(z_after[band, :], 127 - at, 1),
                        ],
                        axis=1,
                    )
                    ahead = jnp.where(at_last, fill, pltpu.roll(field, depth - 1, 1))
                    behind = jnp.where(at_first, fill, pltpu.roll(field, 1, 1))
                    return ahead - behind

                one = second_diff(2) - third_diff(1)
                two = third_diff(0) - first_diff(2)
                three = first_diff(1) - second_diff(0)
                mag = jnp.sqrt(1.0 + 0.25 * (one * one + two * two + three * three))
                both.append(mag)
                for t in range(tiles):
                    turned[t, pl.ds(lo * planes + p, tall, stride=planes), :] = mag[
                        :, t * 128 : (t + 1) * 128
                    ]
            keep_rows(summed, pair * rows + lo, both[0] + both[1])
    level = pair_lanes(pair_rows(summed, planes // 2 * rows // 2)) * 0.125
    level_out[...] = level.reshape(planes // 2, rows // 2, depth // 2)
    size = each * planes
    for m, out in zip(shifts, mags):
        at = pl.multiple_of(size * jnp.bitwise_xor(jnp.bitwise_and(me, 3), m & 3), size)
        for t in range(tiles):
            out[0, t] = turned[t, pl.ds(at, size), :]


def curl(velocity, shifts, pos, halos, level=None):
    _, X, Y, Z = velocity.shape
    H = Y // 2
    each = H // 4
    planes = PLANES
    tiles = Z // 128
    (x_before, x_after), (y_before, y_after), (z_before, z_after) = halos

    def single(comp, shift):
        def index(i, pos):
            at = jnp.minimum(jnp.maximum(i * planes + shift, 0), X - 1)
            return (comp, at, pos[0], 0)

        return pl.BlockSpec((1, 1, H, Z), index)

    plane_spec = pl.BlockSpec((2, H, Z), lambda i, pos: (0, pos[0], 0))
    row_spec = pl.BlockSpec((2, planes, Z), lambda i, pos: (0, i, 0))
    lane_spec = pl.BlockSpec((H, 128), lambda i, pos: (pos[0], 0))
    in_specs = [
        pl.BlockSpec((3, planes, H, Z), lambda i, pos: (0, i, pos[0], 0)),
        single(1, -1),
        single(1, planes),
        single(2, -1),
        single(2, planes),
        pl.BlockSpec((3, planes, 8, Z), lambda i, pos: (0, i, H // 8 - pos[0], 0)),
        plane_spec,
        plane_spec,
        row_spec,
        row_spec,
        lane_spec,
        lane_spec,
    ]
    args = [velocity] * 6 + [x_before, x_after, y_before, y_after, z_before, z_after]
    aliases = {}
    if level is not None:
        in_specs.append(pl.BlockSpec(memory_space=pl.ANY))
        args.append(level)
        aliases = {len(args): len(shifts)}
    mag_spec = pl.BlockSpec((1, tiles, each * planes, 128), lambda i, pos: (i, 0, 0, 0))
    cells = X * H * Z
    return pl.pallas_call(
        functools.partial(curl_kernel, shifts),
        grid_spec=pltpu.PrefetchScalarGridSpec(
            num_scalar_prefetch=1,
            grid=(X // planes,),
            in_specs=in_specs,
            out_specs=[mag_spec] * len(shifts)
            + [pl.BlockSpec((planes // 2, H // 2, Z // 2), lambda i, pos: (i, pos[0], 0))],
            scratch_shapes=[
                pltpu.VMEM((tiles, planes // 2 * H, 128), F32),
                pltpu.VMEM((tiles, planes * H, 128), F32),
            ],
        ),
        out_shape=[jax.ShapeDtypeStruct((X // planes, tiles, each * planes, 128), F32)] * len(shifts)
        + [jax.ShapeDtypeStruct((X // 2, Y // 2, Z // 2), F32)],
        input_output_aliases=aliases,
        cost_estimate=pl.CostEstimate(
            flops=20 * cells, bytes_accessed=20 * cells, transcendentals=cells
        ),
        name="curl",
    )(pos, *args)


def lay_kernel(shifts, pos, *refs):
    count = len(shifts)
    blocks = refs[:count]
    out, placed, sems = refs[-3:]
    _, each, _, depth = placed.shape
    copies = []
    for k, (m, block) in enumerate(zip(shifts, blocks)):
        for b in range(block.shape[0]):
            for t in range(block.shape[1]):
                for y in range(each):
                    placed[k, y, b * 8 : b * 8 + 8, t * 128 : (t + 1) * 128] = block[
                        b, t, y * 8 : y * 8 + 8, :
                    ]
        at = pl.multiple_of(jnp.bitwise_xor(pos[1], m) * depth, depth)
        copy = pltpu.make_async_copy(placed.at[k], out.at[:, :, pl.ds(at, depth)], sems.at[k])
        copy.start()
        copies.append(copy)
    for copy in copies:
        copy.wait()


def lay(blocks, shifts, pos, pencil=None, n=8):
    deep, tiles, rows, width = blocks[0].shape
    X, each, Z = deep * 8, rows // 8, tiles * width
    count = len(shifts)
    vmem = pl.BlockSpec(memory_space=pltpu.VMEM)
    in_specs = [pl.BlockSpec(memory_space=pltpu.SMEM)] + [vmem] * count
    args = [pos, *blocks]
    aliases = {}
    if pencil is not None:
        in_specs.append(pl.BlockSpec(memory_space=pl.ANY))
        args.append(pencil)
        aliases = {count + 1: 0}
    return pl.pallas_call(
        functools.partial(lay_kernel, shifts),
        in_specs=in_specs,
        out_specs=pl.BlockSpec(memory_space=pl.ANY),
        out_shape=jax.ShapeDtypeStruct((each, X, n * Z), F32),
        scratch_shapes=[pltpu.VMEM((count, each, X, Z), F32), pltpu.SemaphoreType.DMA((count,))],
        input_output_aliases=aliases,
        cost_estimate=pl.CostEstimate(
            flops=count * each * X * Z, bytes_accessed=8 * count * each * X * Z, transcendentals=0
        ),
        name="lay",
    )(*args)


def levels_kernel(shifts, pos, *refs):
    blocks = refs[: len(shifts)]
    one, two, three, four, five, s1, s2, s3, s4 = refs[len(shifts) :]
    width = blocks[0].shape[2]
    for m, block in zip(shifts, blocks):
        at = pl.multiple_of(jnp.bitwise_xor(pos[1], m) * width, width)
        one[:, :, pl.ds(at, width)] = block[...]

    def up(planes, scratch):
        half, count = len(planes) // 2, planes[0].shape[0]
        for i in range(half):
            keep_rows(scratch, i * count, planes[2 * i] + planes[2 * i + 1])
        result = pair_lanes(pair_rows(scratch, half * count // 2)) * 0.125
        return [result[i * (count // 2) : (i + 1) * (count // 2), :] for i in range(half)]

    planes = up([one[i] for i in range(one.shape[0])], s1)
    for i, plane in enumerate(planes):
        two[i] = plane
    for target, scratch in ((three, s2), (four, s3), (five, s4)):
        planes = up(planes, scratch)
        for i, plane in enumerate(planes):
            for j in range(plane.shape[0]):
                target[j, i : i + 1, :] = plane[j : j + 1, :]


def levels(blocks, shifts, pos, n=8):
    planes, rows, width = blocks[0].shape
    depth = width * n
    shapes = [(planes >> k, rows >> k, depth >> k) for k in range(5)]
    outs = shapes[:2] + [(r, p, d) for p, r, d in shapes[2:]]
    vmem = pl.BlockSpec(memory_space=pltpu.VMEM)
    return pl.pallas_call(
        functools.partial(levels_kernel, shifts),
        in_specs=[pl.BlockSpec(memory_space=pltpu.SMEM)] + [vmem] * len(blocks),
        out_specs=[vmem] * 5,
        out_shape=[jax.ShapeDtypeStruct(s, F32) for s in outs],
        scratch_shapes=[pltpu.VMEM((s[2] // 128, s[0] // 2 * s[1], 128), F32) for s in shapes[:4]],
        cost_estimate=pl.CostEstimate(
            flops=4 * planes * rows * depth, bytes_accessed=10 * planes * rows * depth, transcendentals=0
        ),
        name="levels",
    )(pos, *blocks)


def swap(value, m):
    return lax.ppermute(value, "gz", [(i, i ^ m) for i in range(lax.axis_size("gz"))])


def exchange(first, last, axis):
    peers = lax.axis_size(axis)
    up = [(i, (i + 1) % peers) for i in range(peers)]
    down = [(j, i) for i, j in up]
    return lax.ppermute(last, axis, up), lax.ppermute(first, axis, down)


def on_device(velocity):
    _, X, _, _ = velocity.shape
    at = lax.axis_index("gz").astype(jnp.int32)
    own = lax.shift_right_logical(at, jnp.int32(2))
    pos_far = jnp.stack([1 - own, at])
    pos_near = jnp.stack([own, at])
    x_halo = exchange(velocity[1:, 0], velocity[1:, X - 1], "gx")
    row_first, row_last, lane_first, lane_last = ends(velocity)
    z_halo = exchange(lane_first, lane_last, "gz")
    y_halo = exchange(row_first, row_last, "gy")
    halos = (x_halo, y_halo, z_halo)
    *far, level = curl(velocity, (4, 5, 6, 7), pos_far, halos)
    *near, level = curl(velocity, (0, 1, 2, 3), pos_near, halos, level)
    levels_by = {0: level}
    levels_by[4] = swap(level, 4)
    levels_by[2] = swap(level, 2)
    levels_by[6] = swap(levels_by[4], 2)
    for m in (0, 4, 2, 6):
        levels_by[m + 1] = swap(levels_by[m], 1)
    got = {0: near[0]}
    for m in range(1, 8):
        got[m] = swap(near[m] if m < 4 else far[m - 4], m)
    upper = levels([levels_by[m] for m in range(8)], tuple(range(8)), pos_near)
    upper = [*upper[:2]] + [jnp.transpose(level, (1, 0, 2)) for level in upper[2:]]
    early, late = EARLY, LATE
    pencil = lay([got[m] for m in early], early, pos_near)
    pencil = lay([got[m] for m in late], late, pos_near, pencil)
    return (jnp.transpose(pencil, (1, 0, 2)), *upper)


EARLY, LATE = (0, 1, 2, 3, 4, 5), (6, 7)


def solution(mesh):
    in_specs = (P(None, "gx", "gy", "gz"),)
    out_specs = (
        P("gx", ("gy", "gz"), None),
        P("gx", "gy", None),
        P("gx", "gy", None),
        P("gx", "gy", None),
        P("gx", "gy", None),
        P("gx", "gy", None),
    )

    return jax.shard_map(
        on_device, mesh=mesh, in_specs=in_specs, out_specs=out_specs, check_vma=False
    )
```

profile of v0, /device:TPU:1, one launch (start us, length us, event | category | flops | bytes accessed | tf_op | source)
XLA Modules:
  0.0 131.6 jit_solution(12781514617484076627)
XLA Ops:
  0.6 1.1 slice_bitcast_fusion
  1.7 2.1 %collective-permute-start = (f32[2,96,256]{2,1,0:T(8,128)S(1)}, f32[2,96,256]{2,1,0:T(8,128)S(1)}, u32[]{:S(2)}, u32[]{:S(2)}) collective-permute-start(f32[2,96,256]{2,1,0:T(8,128)S(1)} %get-tuple-element.45), channel_id=1, source_target_pairs={{0,64},{64,128},{128,192},{192,0},{1,65},{65,129},{129,193},{193,1... | collective-permute-start | bytes 589832 | tf_op jit(solution)/shard_map/ppermute | solution.py:336
  3.8 1.4 %collective-permute-start.1 = (f32[2,96,256]{2,1,0:T(8,128)S(1)}, f32[2,96,256]{2,1,0:T(8,128)S(1)}, u32[]{:S(2)}, u32[]{:S(2)}) collective-permute-start(f32[2,96,256]{2,1,0:T(8,128)S(1)} %get-tuple-element.44), channel_id=1, source_target_pairs={{64,0},{128,64},{192,128},{0,192},{65,1},{129,65},{193,129},{1,193... | collective-permute-start | bytes 589832 | tf_op jit(solution)/shard_map/ppermute | solution.py:336
  5.2 5.3 %ends.1 = (f32[2,32,256]{2,1,0:T(8,128)}, f32[2,32,256]{2,1,0:T(8,128)}, f32[96,128]{1,0:T(8,128)}, f32[96,128]{1,0:T(8,128)}) custom-call(f32[3,32,96,256]{3,2,1,0:T(8,128)} %inner.3, f32[3,32,96,256]{3,2,1,0:T(8,128)} %inner.3, f32[3,32,96,256]{3,2,1,0:T(8,128)} %inner.3), custom_call_target="tpu_custom_call" | custom-call | flops 4000000 | bytes 8000000 | tf_op jit(solution)/shard_map/ends/pallas_call | solution.py:71
  10.4 1.5 %collective-permute-start.2 = (f32[2,32,256]{2,1,0:T(8,128)}, f32[2,32,256]{2,1,0:T(8,128)S(1)}, u32[]{:S(2)}, u32[]{:S(2)}) collective-permute-start(f32[2,32,256]{2,1,0:T(8,128)} %get-tuple-element.25), channel_id=1, source_target_pairs={{0,8},{8,16},{16,24},{24,32},{32,40},{40,48},{48,56},{56,0},{1,9},... | collective-permute-start | bytes 196616 | tf_op jit(solution)/shard_map/ppermute | solution.py:336
  11.9 8.2 %collective-permute-start.3 = (f32[2,32,256]{2,1,0:T(8,128)}, f32[2,32,256]{2,1,0:T(8,128)S(1)}, u32[]{:S(2)}, u32[]{:S(2)}) collective-permute-start(f32[2,32,256]{2,1,0:T(8,128)} %get-tuple-element.26), channel_id=1, source_target_pairs={{8,0},{16,8},{24,16},{32,24},{40,32},{48,40},{56,48},{0,56},{9,1},... | collective-permute-start | bytes 196616 | tf_op jit(solution)/shard_map/ppermute | solution.py:336
  20.1 2.1 %collective-permute-start.4 = (f32[96,128]{1,0:T(8,128)}, f32[96,128]{1,0:T(8,128)S(1)}, u32[]{:S(2)}, u32[]{:S(2)}) collective-permute-start(f32[96,128]{1,0:T(8,128)} %get-tuple-element.27), channel_id=1, source_target_pairs={{0,1},{1,2},{2,3},{3,4},{4,5},{5,6},{6,7},{7,0},{8,9},{9,10},{10,1... | collective-permute-start | bytes 147464 | tf_op jit(solution)/shard_map/ppermute | solution.py:336
  22.2 0.6 pad_add_fusion.pos
  22.8 1.0 collective-permute-done.4.refs_4_
  23.8 4.4 %collective-permute-start.5 = (f32[96,128]{1,0:T(8,128)}, f32[96,128]{1,0:T(8,128)S(1)}, u32[]{:S(2)}, u32[]{:S(2)}) collective-permute-start(f32[96,128]{1,0:T(8,128)} %get-tuple-element.28), channel_id=1, source_target_pairs={{1,0},{2,1},{3,2},{4,3},{5,4},{6,5},{7,6},{0,7},{9,8},{10,9},{11,1... | collective-permute-start | bytes 147464 | tf_op jit(solution)/shard_map/ppermute | solution.py:336
  28.2 0.6 pad_add_fusion.1.pos
  28.8 0.5 collective-permute-done.5.refs_5_
  29.3 0.0 collective-permute-done.2.refs_2_
  29.3 0.0 collective-permute-done.3.refs_3_
  29.3 0.0 copy-start.12
  29.3 0.0 collective-permute-done.refs_0_
  29.3 0.0 copy-start
  29.3 0.0 collective-permute-done.1.refs_1_
  29.3 0.0 copy-done.13
  29.4 0.6 copy-done.14
  29.9 0.0 copy-done.11
  29.9 0.0 copy-done.12
  30.0 0.1 copy-done
  30.0 0.7 copy-done.1
  30.7 7.6 %curl.2 = (f32[4,2,96,128]{3,2,1,0:T(8,128)}, f32[4,2,96,128]{3,2,1,0:T(8,128)}, f32[4,2,96,128]{3,2,1,0:T(8,128)}, f32[4,2,96,128]{3,2,1,0:T(8,128)}, f32[16,48,128]{2,1,0:T(8,128)}) custom-call(s32[2]{0:T(128)} %pad_add_fusion.1.pos, f32[3,32,96,256]{3,2,1,0:T(8,128)} %inner.3, f32[3,32,96,256]{3,2,1,0:T(8,128)} %inner.3, f32[3,32,96,256]{3,2,1,0:T(8,128)} %inner.3, ...), custom_call_target="tpu_custom_call" | custom-call | flops 7864320 | bytes 7864320 | tf_op jit(solution)/shard_map/curl/pallas_call | solution.py:214
  38.3 4.1 %collective-permute-start.6 = (f32[4,2,96,128]{3,2,1,0:T(8,128)}, f32[4,2,96,128]{3,2,1,0:T(8,128)S(1)}, u32[]{:S(2)}, u32[]{:S(2)}) collective-permute-start(f32[4,2,96,128]{3,2,1,0:T(8,128)} %get-tuple-element.29), channel_id=1, source_target_pairs={{0,6},{1,7},{2,4},{3,5},{4,2},{5,3},{6,0},{7,1},{8,14},{9,15},{10,... | collective-permute-start | bytes 1179656 | tf_op jit(solution)/shard_map/ppermute | solution.py:329
  42.5 7.8 %curl.3 = (f32[4,2,96,128]{3,2,1,0:T(8,128)}, f32[4,2,96,128]{3,2,1,0:T(8,128)}, f32[4,2,96,128]{3,2,1,0:T(8,128)}, f32[4,2,96,128]{3,2,1,0:T(8,128)}, f32[16,48,128]{2,1,0:T(8,128)}) custom-call(s32[2]{0:T(128)} %pad_add_fusion.pos, f32[3,32,96,256]{3,2,1,0:T(8,128)} %inner.3, f32[3,32,96,256]{3,2,1,0:T(8,128)} %inner.3, ...), custom_call_target="tpu_custom_call", output_to_operand_aliasing={{4}: (13, {})} | custom-call | flops 7864320 | bytes 7864320 | tf_op jit(solution)/shard_map/curl/pallas_call | solution.py:214
  50.2 0.1 collective-permute-start.8
  50.3 0.1 collective-permute-start.9
  50.4 0.7 collective-permute-start.16
  51.1 1.4 %collective-permute-start.10 = (f32[4,2,96,128]{3,2,1,0:T(8,128)}, f32[4,2,96,128]{3,2,1,0:T(8,128)S(1)}, u32[]{:S(2)}, u32[]{:S(2)}) collective-permute-start(f32[4,2,96,128]{3,2,1,0:T(8,128)} %get-tuple-element.35), channel_id=1, source_target_pairs={{0,3},{1,2},{2,1},{3,0},{4,7},{5,6},{6,5},{7,4},{8,11},{9,10},{10,... | collective-permute-start | bytes 1179656 | tf_op jit(solution)/shard_map/ppermute | solution.py:329
  52.5 0.0 collective-permute-done.6.refs_0_
  52.5 0.0 copy-done.15
  52.5 6.8 %collective-permute-start.11 = (f32[4,2,96,128]{3,2,1,0:T(8,128)S(1)}, f32[4,2,96,128]{3,2,1,0:T(8,128)S(1)}, u32[]{:S(2)}, u32[]{:S(2)}) collective-permute-start(f32[4,2,96,128]{3,2,1,0:T(8,128)S(1)} %copy-done.15), channel_id=1, source_target_pairs={{0,4},{1,5},{2,6},{3,7},{4,0},{5,1},{6,2},{7,3},{8,12},{9,13},{10,... | collective-permute-start | bytes 1179656 | tf_op jit(solution)/shard_map/ppermute | solution.py:329
  59.2 0.0 collective-permute-done.8.refs_1_
  59.2 0.4 collective-permute-start.12
  59.6 4.6 %collective-permute-done.9.refs_2_ = f32[4,2,96,128]{3,2,1,0:T(8,128)S(1)} collective-permute-done((f32[4,2,96,128]{3,2,1,0:T(8,128)}, f32[4,2,96,128]{3,2,1,0:T(8,128)S(1)}, u32[]{:S(2)}, u32[]{:S(2)}) %collective-permute-start.9) | collective-permute-done | bytes 393248 | tf_op jit(solution)/shard_map/ppermute | solution.py:329
  64.3 0.0 collective-permute-start.14
  64.3 11.4 %collective-permute-done.16.refs_4_ = f32[16,48,128]{2,1,0:T(8,128)S(1)} collective-permute-done((f32[16,48,128]{2,1,0:T(8,128)}, f32[16,48,128]{2,1,0:T(8,128)S(1)}, u32[]{:S(2)}, u32[]{:S(2)}) %collective-permute-start.16) | collective-permute-done | bytes 393248 | tf_op jit(solution)/shard_map/ppermute | solution.py:329
  75.7 0.0 collective-permute-start.18
  75.7 7.2 %collective-permute-done.10.refs_3_ = f32[4,2,96,128]{3,2,1,0:T(8,128)S(1)} collective-permute-done((f32[4,2,96,128]{3,2,1,0:T(8,128)}, f32[4,2,96,128]{3,2,1,0:T(8,128)S(1)}, u32[]{:S(2)}, u32[]{:S(2)}) %collective-permute-start.10) | collective-permute-done | bytes 393248 | tf_op jit(solution)/shard_map/ppermute | solution.py:329
  82.9 0.0 collective-permute-start.13
  82.9 17.9 %collective-permute-done.11.refs_4_ = f32[4,2,96,128]{3,2,1,0:T(8,128)S(1)} collective-permute-done((f32[4,2,96,128]{3,2,1,0:T(8,128)S(1)}, f32[4,2,96,128]{3,2,1,0:T(8,128)S(1)}, u32[]{:S(2)}, u32[]{:S(2)}) %collective-permute-start.11) | collective-permute-done | bytes 393248 | tf_op jit(solution)/shard_map/ppermute | solution.py:329
  100.7 2.0 %collective-permute-start.7 = (f32[4,2,96,128]{3,2,1,0:T(8,128)}, f32[4,2,96,128]{3,2,1,0:T(8,128)S(1)}, u32[]{:S(2)}, u32[]{:S(2)}) collective-permute-start(f32[4,2,96,128]{3,2,1,0:T(8,128)} %get-tuple-element.30), channel_id=1, source_target_pairs={{0,7},{1,6},{2,5},{3,4},{4,3},{5,2},{6,1},{7,0},{8,15},{9,14},{10,... | collective-permute-start | bytes 1179656 | tf_op jit(solution)/shard_map/ppermute | solution.py:329
  102.7 4.2 %collective-permute-done.12.refs_5_ = f32[4,2,96,128]{3,2,1,0:T(8,128)S(1)} collective-permute-done((f32[4,2,96,128]{3,2,1,0:T(8,128)}, f32[4,2,96,128]{3,2,1,0:T(8,128)S(1)}, u32[]{:S(2)}, u32[]{:S(2)}) %collective-permute-start.12) | collective-permute-done | bytes 393248 | tf_op jit(solution)/shard_map/ppermute | solution.py:329
  107.0 2.8 %collective-permute-start.17 = (f32[16,48,128]{2,1,0:T(8,128)S(1)}, f32[16,48,128]{2,1,0:T(8,128)}, u32[]{:S(2)}, u32[]{:S(2)}) collective-permute-start(f32[16,48,128]{2,1,0:T(8,128)S(1)} %collective-permute-done.16.refs_4_), channel_id=1, source_target_pairs={{0,1},{1,0},{2,3},{3,2},{4,5},{5,4},{6,7},{7,6},{8,9},{9,8},{10,11... | collective-permute-start | bytes 1179656 | tf_op jit(solution)/shard_map/ppermute | solution.py:329
  109.8 0.0 collective-permute-done.14.refs_2_
  109.8 0.1 collective-permute-start.15
  109.9 1.8 %collective-permute-done.18.refs_6_ = f32[16,48,128]{2,1,0:T(8,128)} collective-permute-done((f32[16,48,128]{2,1,0:T(8,128)S(1)}, f32[16,48,128]{2,1,0:T(8,128)}, u32[]{:S(2)}, u32[]{:S(2)}) %collective-permute-start.18) | collective-permute-done | bytes 393248 | tf_op jit(solution)/shard_map/ppermute | solution.py:329
  111.7 9.6 %collective-permute-start.19 = (f32[16,48,128]{2,1,0:T(8,128)}, f32[16,48,128]{2,1,0:T(8,128)}, u32[]{:S(2)}, u32[]{:S(2)}) collective-permute-start(f32[16,48,128]{2,1,0:T(8,128)} %collective-permute-done.18.refs_6_), channel_id=1, source_target_pairs={{0,1},{1,0},{2,3},{3,2},{4,5},{5,4},{6,7},{7,6},{8,9},{9,8},{10,11... | collective-permute-start | bytes 1179656 | tf_op jit(solution)/shard_map/ppermute | solution.py:329
  121.2 0.0 copy-done.4
  121.2 0.0 copy-done.5
  121.3 0.0 copy-done.6
  121.3 0.0 copy-done.7
  121.3 3.1 %lay.2.refs_2_ = f32[12,32,2048]{2,1,0:T(8,128)} custom-call(s32[2]{0:T(128)} %pad_add_fusion.pos, f32[4,2,96,128]{3,2,1,0:T(8,128)} %get-tuple-element.32.refs_0_, f32[4,2,96,128]{3,2,1,0:T(8,128)} %copy-done.4, f32[4,2,96,128]{3,2,1,0:T(8,128)} %copy-done.5, f32[4,2,96,128]{3,2,1,0:T(8,128)} %copy-done.6, f32[4,2,96,128]{3,2,1,0:T(8,128)} %copy-done.7, ...), custom_call_target="tpu_custom_call" | custom-call | flops 589824 | bytes 4718592 | tf_op jit(solution)/shard_map/lay/pallas_call | solution.py:270
  124.4 0.0 collective-permute-done.7.refs_1_
  124.4 0.0 copy-start.3
  124.4 0.7 copy-done.3
  125.1 2.0 %lay.3 = f32[12,32,2048]{2,1,0:T(8,128)} custom-call(s32[2]{0:T(128)} %pad_add_fusion.pos, f32[4,2,96,128]{3,2,1,0:T(8,128)} %copy-done.2, f32[4,2,96,128]{3,2,1,0:T(8,128)} %copy-done.3, f32[12,32,2048]{2,1,0:T(8,128)} %lay.2.refs_2_), custom_call_target="tpu_custom_call", output_to_operand_aliasing={{}: (3, {})} | custom-call | flops 196608 | bytes 1572864 | tf_op jit(solution)/shard_map/lay/pallas_call | solution.py:270
  127.2 0.0 collective-permute-done.13.refs_1_
  127.2 0.0 collective-permute-done.15.refs_3_
  127.2 0.0 collective-permute-done.17.refs_5_
  127.2 0.0 collective-permute-done.19.refs_7_
  127.2 4.3 %levels.1 = (f32[16,48,1024]{2,1,0:T(8,128)}, f32[8,24,512]{2,1,0:T(8,128)}, f32[12,4,256]{2,1,0:T(4,128)}, f32[6,2,128]{2,1,0:T(2,128)}, f32[3,1,64]{2,1,0:T(1,128)}) custom-call(s32[2]{0:T(128)} %pad_add_fusion.pos, f32[16,48,128]{2,1,0:T(8,128)} %get-tuple-element.38.refs_0_, f32[16,48,128]{2,1,0:T(8,128)} %collective-permute-done.13.refs_1_, ...), custom_call_target="tpu_custom_call" | custom-call | flops 3145728 | bytes 7864320 | tf_op jit(solution)/shard_map/levels/pallas_call | solution.py:315
  (17 shorter events, 0.0 us)
Async XLA Ops:
  1.7 27.6 %collective-permute-start = (f32[2,96,256]{2,1,0:T(8,128)S(1)}, f32[2,96,256]{2,1,0:T(8,128)S(1)}, u32[]{:S(2)}, u32[]{:S(2)}) collective-permute-start(f32[2,96,256]{2,1,0:T(8,128)S(1)} %get-tuple-element.45), channel_id=1, source_target_pairs={{0,64},{64,128},{128,192},{192,0},{1,65},{65,129},{129,193},{193,1... | collective-permute-start | bytes 589832 | tf_op jit(solution)/shard_map/ppermute | solution.py:336
  3.8 25.5 %collective-permute-start.1 = (f32[2,96,256]{2,1,0:T(8,128)S(1)}, f32[2,96,256]{2,1,0:T(8,128)S(1)}, u32[]{:S(2)}, u32[]{:S(2)}) collective-permute-start(f32[2,96,256]{2,1,0:T(8,128)S(1)} %get-tuple-element.44), channel_id=1, source_target_pairs={{64,0},{128,64},{192,128},{0,192},{65,1},{129,65},{193,129},{1,193... | collective-permute-start | bytes 589832 | tf_op jit(solution)/shard_map/ppermute | solution.py:336
  10.4 18.9 %collective-permute-start.2 = (f32[2,32,256]{2,1,0:T(8,128)}, f32[2,32,256]{2,1,0:T(8,128)S(1)}, u32[]{:S(2)}, u32[]{:S(2)}) collective-permute-start(f32[2,32,256]{2,1,0:T(8,128)} %get-tuple-element.25), channel_id=1, source_target_pairs={{0,8},{8,16},{16,24},{24,32},{32,40},{40,48},{48,56},{56,0},{1,9},... | collective-permute-start | bytes 196616 | tf_op jit(solution)/shard_map/ppermute | solution.py:336
  11.9 17.4 %collective-permute-start.3 = (f32[2,32,256]{2,1,0:T(8,128)}, f32[2,32,256]{2,1,0:T(8,128)S(1)}, u32[]{:S(2)}, u32[]{:S(2)}) collective-permute-start(f32[2,32,256]{2,1,0:T(8,128)} %get-tuple-element.26), channel_id=1, source_target_pairs={{8,0},{16,8},{24,16},{32,24},{40,32},{48,40},{56,48},{0,56},{9,1},... | collective-permute-start | bytes 196616 | tf_op jit(solution)/shard_map/ppermute | solution.py:336
  20.1 3.8 %collective-permute-start.4 = (f32[96,128]{1,0:T(8,128)}, f32[96,128]{1,0:T(8,128)S(1)}, u32[]{:S(2)}, u32[]{:S(2)}) collective-permute-start(f32[96,128]{1,0:T(8,128)} %get-tuple-element.27), channel_id=1, source_target_pairs={{0,1},{1,2},{2,3},{3,4},{4,5},{5,6},{6,7},{7,0},{8,9},{9,10},{10,1... | collective-permute-start | bytes 147464 | tf_op jit(solution)/shard_map/ppermute | solution.py:336
  23.8 5.5 %copy-start.13 = (f32[96,128]{1,0:T(8,128)}, f32[96,128]{1,0:T(8,128)S(1)}, u32[]{:S(2)}) copy-start(f32[96,128]{1,0:T(8,128)S(1)} %collective-permute-done.4.refs_4_) | copy-start | bytes 147460
  23.8 5.5 %collective-permute-start.5 = (f32[96,128]{1,0:T(8,128)}, f32[96,128]{1,0:T(8,128)S(1)}, u32[]{:S(2)}, u32[]{:S(2)}) collective-permute-start(f32[96,128]{1,0:T(8,128)} %get-tuple-element.28), channel_id=1, source_target_pairs={{1,0},{2,1},{3,2},{4,3},{5,4},{6,5},{7,6},{0,7},{9,8},{10,9},{11,1... | collective-permute-start | bytes 147464 | tf_op jit(solution)/shard_map/ppermute | solution.py:336
  29.3 0.6 copy-start.14
  29.3 0.6 copy-start.11
  29.3 0.7 copy-start.12
  29.3 0.7 copy-start
  30.0 0.7 copy-start.1
  38.3 14.1 %collective-permute-start.6 = (f32[4,2,96,128]{3,2,1,0:T(8,128)}, f32[4,2,96,128]{3,2,1,0:T(8,128)S(1)}, u32[]{:S(2)}, u32[]{:S(2)}) collective-permute-start(f32[4,2,96,128]{3,2,1,0:T(8,128)} %get-tuple-element.29), channel_id=1, source_target_pairs={{0,6},{1,7},{2,4},{3,5},{4,2},{5,3},{6,0},{7,1},{8,14},{9,15},{10,... | collective-permute-start | bytes 1179656 | tf_op jit(solution)/shard_map/ppermute | solution.py:329
  42.5 10.0 %copy-start.15 = (f32[4,2,96,128]{3,2,1,0:T(8,128)S(1)}, f32[4,2,96,128]{3,2,1,0:T(8,128)}, u32[]{:S(2)}) copy-start(f32[4,2,96,128]{3,2,1,0:T(8,128)} %get-tuple-element.36) | copy-start | bytes 1179652
  50.2 9.0 %collective-permute-start.8 = (f32[4,2,96,128]{3,2,1,0:T(8,128)}, f32[4,2,96,128]{3,2,1,0:T(8,128)S(1)}, u32[]{:S(2)}, u32[]{:S(2)}) collective-permute-start(f32[4,2,96,128]{3,2,1,0:T(8,128)} %get-tuple-element.33), channel_id=1, source_target_pairs={{0,1},{1,0},{2,3},{3,2},{4,5},{5,4},{6,7},{7,6},{8,9},{9,8},{10,11... | collective-permute-start | bytes 1179656 | tf_op jit(solution)/shard_map/ppermute | solution.py:329
  50.3 13.9 %collective-permute-start.9 = (f32[4,2,96,128]{3,2,1,0:T(8,128)}, f32[4,2,96,128]{3,2,1,0:T(8,128)S(1)}, u32[]{:S(2)}, u32[]{:S(2)}) collective-permute-start(f32[4,2,96,128]{3,2,1,0:T(8,128)} %get-tuple-element.34), channel_id=1, source_target_pairs={{0,2},{1,3},{2,0},{3,1},{4,6},{5,7},{6,4},{7,5},{8,10},{9,11},{10,... | collective-permute-start | bytes 1179656 | tf_op jit(solution)/shard_map/ppermute | solution.py:329
  50.4 25.2 %collective-permute-start.16 = (f32[16,48,128]{2,1,0:T(8,128)}, f32[16,48,128]{2,1,0:T(8,128)S(1)}, u32[]{:S(2)}, u32[]{:S(2)}) collective-permute-start(f32[16,48,128]{2,1,0:T(8,128)} %get-tuple-element.38.refs_0_), channel_id=1, source_target_pairs={{0,4},{1,5},{2,6},{3,7},{4,0},{5,1},{6,2},{7,3},{8,12},{9,13},{10,... | collective-permute-start | bytes 1179656 | tf_op jit(solution)/shard_map/ppermute | solution.py:329
  51.1 31.8 %collective-permute-start.10 = (f32[4,2,96,128]{3,2,1,0:T(8,128)}, f32[4,2,96,128]{3,2,1,0:T(8,128)S(1)}, u32[]{:S(2)}, u32[]{:S(2)}) collective-permute-start(f32[4,2,96,128]{3,2,1,0:T(8,128)} %get-tuple-element.35), channel_id=1, source_target_pairs={{0,3},{1,2},{2,1},{3,0},{4,7},{5,6},{6,5},{7,4},{8,11},{9,10},{10,... | collective-permute-start | bytes 1179656 | tf_op jit(solution)/shard_map/ppermute | solution.py:329
  52.5 71.9 %copy-start.2 = (f32[4,2,96,128]{3,2,1,0:T(8,128)}, f32[4,2,96,128]{3,2,1,0:T(8,128)S(1)}, u32[]{:S(2)}) copy-start(f32[4,2,96,128]{3,2,1,0:T(8,128)S(1)} %collective-permute-done.6.refs_0_) | copy-start | bytes 1179652
  52.5 48.3 %collective-permute-start.11 = (f32[4,2,96,128]{3,2,1,0:T(8,128)S(1)}, f32[4,2,96,128]{3,2,1,0:T(8,128)S(1)}, u32[]{:S(2)}, u32[]{:S(2)}) collective-permute-start(f32[4,2,96,128]{3,2,1,0:T(8,128)S(1)} %copy-done.15), channel_id=1, source_target_pairs={{0,4},{1,5},{2,6},{3,7},{4,0},{5,1},{6,2},{7,3},{8,12},{9,13},{10,... | collective-permute-start | bytes 1179656 | tf_op jit(solution)/shard_map/ppermute | solution.py:329
  59.2 62.0 %copy-start.4 = (f32[4,2,96,128]{3,2,1,0:T(8,128)}, f32[4,2,96,128]{3,2,1,0:T(8,128)S(1)}, u32[]{:S(2)}) copy-start(f32[4,2,96,128]{3,2,1,0:T(8,128)S(1)} %collective-permute-done.8.refs_1_) | copy-start | bytes 1179652
  59.2 47.7 %collective-permute-start.12 = (f32[4,2,96,128]{3,2,1,0:T(8,128)}, f32[4,2,96,128]{3,2,1,0:T(8,128)S(1)}, u32[]{:S(2)}, u32[]{:S(2)}) collective-permute-start(f32[4,2,96,128]{3,2,1,0:T(8,128)} %get-tuple-element.37), channel_id=1, source_target_pairs={{0,5},{1,4},{2,7},{3,6},{4,1},{5,0},{6,3},{7,2},{8,13},{9,12},{10,... | collective-permute-start | bytes 1179656 | tf_op jit(solution)/shard_map/ppermute | solution.py:329
  64.3 57.0 %copy-start.5 = (f32[4,2,96,128]{3,2,1,0:T(8,128)}, f32[4,2,96,128]{3,2,1,0:T(8,128)S(1)}, u32[]{:S(2)}) copy-start(f32[4,2,96,128]{3,2,1,0:T(8,128)S(1)} %collective-permute-done.9.refs_2_) | copy-start | bytes 1179652
  64.3 45.5 %collective-permute-start.14 = (f32[16,48,128]{2,1,0:T(8,128)}, f32[16,48,128]{2,1,0:T(8,128)S(1)}, u32[]{:S(2)}, u32[]{:S(2)}) collective-permute-start(f32[16,48,128]{2,1,0:T(8,128)} %get-tuple-element.38.refs_0_), channel_id=1, source_target_pairs={{0,2},{1,3},{2,0},{3,1},{4,6},{5,7},{6,4},{7,5},{8,10},{9,11},{10,... | collective-permute-start | bytes 1179656 | tf_op jit(solution)/shard_map/ppermute | solution.py:329
  75.7 51.6 %copy-start.9 = (f32[16,48,128]{2,1,0:T(8,128)}, f32[16,48,128]{2,1,0:T(8,128)S(1)}, u32[]{:S(2)}) copy-start(f32[16,48,128]{2,1,0:T(8,128)S(1)} %collective-permute-done.16.refs_4_) | copy-start | bytes 1179652
  75.7 36.0 %collective-permute-start.18 = (f32[16,48,128]{2,1,0:T(8,128)S(1)}, f32[16,48,128]{2,1,0:T(8,128)}, u32[]{:S(2)}, u32[]{:S(2)}) collective-permute-start(f32[16,48,128]{2,1,0:T(8,128)S(1)} %collective-permute-done.16.refs_4_), channel_id=1, source_target_pairs={{0,2},{1,3},{2,0},{3,1},{4,6},{5,7},{6,4},{7,5},{8,10},{9,11},{10,... | collective-permute-start | bytes 1179656 | tf_op jit(solution)/shard_map/ppermute | solution.py:329
  82.8 38.4 %copy-start.6 = (f32[4,2,96,128]{3,2,1,0:T(8,128)}, f32[4,2,96,128]{3,2,1,0:T(8,128)S(1)}, u32[]{:S(2)}) copy-start(f32[4,2,96,128]{3,2,1,0:T(8,128)S(1)} %collective-permute-done.10.refs_3_) | copy-start | bytes 1179652
  82.9 44.3 %collective-permute-start.13 = (f32[16,48,128]{2,1,0:T(8,128)}, f32[16,48,128]{2,1,0:T(8,128)}, u32[]{:S(2)}, u32[]{:S(2)}) collective-permute-start(f32[16,48,128]{2,1,0:T(8,128)} %get-tuple-element.38.refs_0_), channel_id=1, source_target_pairs={{0,1},{1,0},{2,3},{3,2},{4,5},{5,4},{6,7},{7,6},{8,9},{9,8},{10,11... | collective-permute-start | bytes 1179656 | tf_op jit(solution)/shard_map/ppermute | solution.py:329
  100.7 20.5 %copy-start.7 = (f32[4,2,96,128]{3,2,1,0:T(8,128)}, f32[4,2,96,128]{3,2,1,0:T(8,128)S(1)}, u32[]{:S(2)}) copy-start(f32[4,2,96,128]{3,2,1,0:T(8,128)S(1)} %collective-permute-done.11.refs_4_) | copy-start | bytes 1179652
  100.7 23.6 %collective-permute-start.7 = (f32[4,2,96,128]{3,2,1,0:T(8,128)}, f32[4,2,96,128]{3,2,1,0:T(8,128)S(1)}, u32[]{:S(2)}, u32[]{:S(2)}) collective-permute-start(f32[4,2,96,128]{3,2,1,0:T(8,128)} %get-tuple-element.30), channel_id=1, source_target_pairs={{0,7},{1,6},{2,5},{3,4},{4,3},{5,2},{6,1},{7,0},{8,15},{9,14},{10,... | collective-permute-start | bytes 1179656 | tf_op jit(solution)/shard_map/ppermute | solution.py:329
  107.0 14.3 %copy-start.8 = (f32[4,2,96,128]{3,2,1,0:T(8,128)}, f32[4,2,96,128]{3,2,1,0:T(8,128)S(1)}, u32[]{:S(2)}) copy-start(f32[4,2,96,128]{3,2,1,0:T(8,128)S(1)} %collective-permute-done.12.refs_5_) | copy-start | bytes 1179652
  107.0 20.2 %collective-permute-start.17 = (f32[16,48,128]{2,1,0:T(8,128)S(1)}, f32[16,48,128]{2,1,0:T(8,128)}, u32[]{:S(2)}, u32[]{:S(2)}) collective-permute-start(f32[16,48,128]{2,1,0:T(8,128)S(1)} %collective-permute-done.16.refs_4_), channel_id=1, source_target_pairs={{0,1},{1,0},{2,3},{3,2},{4,5},{5,4},{6,7},{7,6},{8,9},{9,8},{10,11... | collective-permute-start | bytes 1179656 | tf_op jit(solution)/shard_map/ppermute | solution.py:329
  109.8 17.4 %copy-start.10 = (f32[16,48,128]{2,1,0:T(8,128)}, f32[16,48,128]{2,1,0:T(8,128)S(1)}, u32[]{:S(2)}) copy-start(f32[16,48,128]{2,1,0:T(8,128)S(1)} %collective-permute-done.14.refs_2_) | copy-start | bytes 1179652
  109.8 17.4 %collective-permute-start.15 = (f32[16,48,128]{2,1,0:T(8,128)S(1)}, f32[16,48,128]{2,1,0:T(8,128)}, u32[]{:S(2)}, u32[]{:S(2)}) collective-permute-start(f32[16,48,128]{2,1,0:T(8,128)S(1)} %collective-permute-done.14.refs_2_), channel_id=1, source_target_pairs={{0,1},{1,0},{2,3},{3,2},{4,5},{5,4},{6,7},{7,6},{8,9},{9,8},{10,11... | collective-permute-start | bytes 1179656 | tf_op jit(solution)/shard_map/ppermute | solution.py:329
  111.7 15.5 %collective-permute-start.19 = (f32[16,48,128]{2,1,0:T(8,128)}, f32[16,48,128]{2,1,0:T(8,128)}, u32[]{:S(2)}, u32[]{:S(2)}) collective-permute-start(f32[16,48,128]{2,1,0:T(8,128)} %collective-permute-done.18.refs_6_), channel_id=1, source_target_pairs={{0,1},{1,0},{2,3},{3,2},{4,5},{5,4},{6,7},{7,6},{8,9},{9,8},{10,11... | collective-permute-start | bytes 1179656 | tf_op jit(solution)/shard_map/ppermute | solution.py:329
  124.4 0.7 copy-start.3
where the time goes:
time: 132 us
  waiting for transfers between devices  48.7 us (37%)
  starting transfers between devices  47.6 us (36%)
  Pallas kernels  30.1 us (23%)
  local copies, waits for them, and re-layouts  3.2 us (2%)
    ppermute x14, waiting for transfers between devices, swap(): lax.ppermute(value, 'gz', [(i, i ^ m) for i in range(lax.axis_size('gz'))])  47.1 us
    ppermute x14, starting transfers between devices, swap(): lax.ppermute(value, 'gz', [(i, i ^ m) for i in range(lax.axis_size('gz'))])  28 us
    ppermute x6, starting transfers between devices, exchange(): return (lax.ppermute(last, axis, up), lax.ppermute(first, axis, down))  19.6 us
    pallas_call x2, Pallas kernels, curl(): pl.pallas_call(functools.partial(curl_kernel, shifts), grid_spec=pltpu.Pr...  15.4 us
    pallas_call x1, Pallas kernels, ends(): pl.pallas_call(ends_kernel, grid=(X // PLANES,), in_specs=[pl.BlockSpec((...  5.27 us
    pallas_call x2, Pallas kernels, lay(): pl.pallas_call(functools.partial(lay_kernel, shifts), in_specs=in_specs,...  5.12 us
    pallas_call x1, Pallas kernels, levels(): pl.pallas_call(functools.partial(levels_kernel, shifts), in_specs=[pl.Blo...  4.32 us
  transfers between devices with their start and end apart: 20, of which 8 were waited for; matrix products, arithmetic and copies ran while one was open for 1% of the time, Pallas kernels for 14%

commit v1 on v0

v1 whole, which is shorter than its diff:
```python
import functools

import jax
import jax.numpy as jnp
from jax import lax
from jax.experimental import pallas as pl
from jax.experimental.pallas import tpu as pltpu
from jax.sharding import PartitionSpec as P


PLANES = 8
HIGHEST = lax.Precision.HIGHEST
F32 = jnp.float32


def pairing(depth):
    row = lax.broadcasted_iota(jnp.int32, (depth, depth // 2), 0)
    col = lax.broadcasted_iota(jnp.int32, (depth, depth // 2), 1)
    return (lax.div(row, jnp.int32(2)) == col).astype(F32)


def pair_lanes(value):
    _, depth = value.shape
    width = min(depth, 256)
    matrix = pairing(width)
    parts = [
        jnp.dot(value[:, i : i + width], matrix, precision=HIGHEST, preferred_element_type=F32)
        for i in range(0, depth, width)
    ]
    return parts[0] if len(parts) == 1 else jnp.concatenate(parts, axis=1)


def keep_rows(scratch, at, value):
    for t in range(scratch.shape[0]):
        scratch[t, at : at + value.shape[0], :] = value[:, t * 128 : (t + 1) * 128]


def pair_rows(scratch, pairs):
    parts = [
        scratch[t, pl.ds(0, pairs, stride=2), :] + scratch[t, pl.ds(1, pairs, stride=2), :]
        for t in range(scratch.shape[0])
    ]
    return parts[0] if len(parts) == 1 else jnp.concatenate(parts, axis=1)


def edges_kernel(v0, v1, w0, w1, ut, ub, wt, wb, x_first, x_last, y_first, y_last):
    for k, (first, last) in enumerate(((v0, v1), (w0, w1))):
        x_first[k] = first[0, 0]
        x_last[k] = last[0, 0]
    for k, (top, bottom) in enumerate(((ut, ub), (wt, wb))):
        for p in range(top.shape[1]):
            y_first[k, p : p + 1, :] = top[0, p, 0:1, :]
            y_last[k, p : p + 1, :] = bottom[0, p, 7:8, :]


def edges(velocity):
    _, X, Y, Z = velocity.shape

    def plane(comp, at):
        return pl.BlockSpec((1, 1, Y, Z), lambda i: (comp, at, 0, 0))

    def rows(comp, at):
        return pl.BlockSpec((1, X, 8, Z), lambda i: (comp, 0, at, 0))

    planes = jax.ShapeDtypeStruct((2, Y, Z), F32)
    lines = jax.ShapeDtypeStruct((2, X, Z), F32)
    return pl.pallas_call(
        edges_kernel,
        grid=(1,),
        in_specs=[plane(1, 0), plane(1, X - 1), plane(2, 0), plane(2, X - 1)]
        + [rows(0, 0), rows(0, Y // 8 - 1), rows(2, 0), rows(2, Y // 8 - 1)],
        out_specs=[pl.BlockSpec(s.shape, lambda i: (0, 0, 0)) for s in (planes, planes, lines, lines)],
        out_shape=[planes, planes, lines, lines],
        cost_estimate=pl.CostEstimate(flops=1_000_000, bytes_accessed=2_000_000, transcendentals=0),
        name="edges",
    )(*[velocity] * 8)


def lanes_at(k, x):
    last = 2 * (k * 32 + x)
    return last, lax.rem(last + 127, 128)


def ends_kernel(vel, lane_first, lane_last):
    step = pl.program_id(0)
    _, planes, rows, depth = vel.shape
    lane = lax.broadcasted_iota(jnp.int32, (rows, 128), 1)
    first = lane_first[...]
    last = lane_last[...]
    for k in range(2):
        for p in range(planes):
            to_last, to_first = lanes_at(k, step * planes + p)
            first = jnp.where(
                lane == to_first, pltpu.roll(vel[k, p, :, :128], to_first, 1), first
            )
            last = jnp.where(
                lane == to_last, pltpu.roll(vel[k, p, :, depth - 128 :], to_last + 1, 1), last
            )
    lane_first[...] = first
    lane_last[...] = last


def ends(velocity):
    _, X, Y, Z = velocity.shape
    lanes = jax.ShapeDtypeStruct((Y, 128), F32)
    spec = pl.BlockSpec((Y, 128), lambda i: (0, 0))
    return pl.pallas_call(
        ends_kernel,
        grid=(X // PLANES,),
        in_specs=[pl.BlockSpec((2, PLANES, Y, Z), lambda i: (0, i, 0, 0))],
        out_specs=[spec, spec],
        out_shape=[lanes, lanes],
        cost_estimate=pl.CostEstimate(flops=4_000_000, bytes_accessed=7_000_000, transcendentals=0),
        name="ends",
    )(velocity)


def curl_kernel(shifts, each, with_level, pos, vel, v_before, v_after, w_before, w_after, *refs):
    above, below, x_before, x_after, y_before, y_after, z_before, z_after = refs[:8]
    count = len(shifts)
    if with_level:
        level_out, turned, summed = refs[-3:]
        mags = refs[-3 - count : -3]
    else:
        turned = refs[-1]
        mags = refs[-1 - count : -1]
    band_at, me, bands = pos[0], pos[1], pos[2]
    step = pl.program_id(0)
    _, planes, rows, depth = vel.shape
    tall = 2 * each
    tiles = depth // 128
    lane = lax.broadcasted_iota(jnp.int32, (tall, depth), 1)
    at_first, at_last = lane == 0, lane == depth - 1
    even_lane = lax.broadcasted_iota(jnp.int32, (tall, 128), 1) % 2 == 0
    at_top, at_bottom = band_at == 0, band_at == bands - 1
    at_start = step == 0
    at_end = step == pl.num_programs(0) - 1

    for pair in range(planes // 2):
        for q in range(rows // tall):
            lo, hi = q * tall, (q + 1) * tall
            band = slice(lo, hi)
            both = []
            fills = jnp.where(even_lane, z_before[band, :], z_after[band, :])
            for p in (2 * pair, 2 * pair + 1):

                def first_diff(k):
                    if p + 1 < planes:
                        ahead = vel[k, p + 1, band, :]
                    else:
                        near = (v_after, w_after)[k - 1][0, 0, band, :]
                        ahead = jnp.where(at_end, x_after[k - 1, band, :], near)
                    if p > 0:
                        behind = vel[k, p - 1, band, :]
                    else:
                        near = (v_before, w_before)[k - 1][0, 0, band, :]
                        behind = jnp.where(at_start, x_before[k - 1, band, :], near)
                    return ahead - behind

                def second_diff(k):
                    slot = 0 if k == 0 else 1
                    if lo == 0:
                        edge = jnp.where(at_top, y_before[slot, p : p + 1, :], above[k, p, 7:8, :])
                        behind = jnp.concatenate([edge, vel[k, p, 0 : hi - 1, :]], axis=0)
                    else:
                        behind = vel[k, p, lo - 1 : hi - 1, :]
                    if hi == rows:
                        edge = jnp.where(at_bottom, y_after[slot, p : p + 1, :], below[k, p, 0:1, :])
                        ahead = jnp.concatenate([vel[k, p, lo + 1 : hi, :], edge], axis=0)
                    else:
                        ahead = vel[k, p, lo + 1 : hi + 1, :]
                    return ahead - behind

                def third_diff(k):
                    field = vel[k, p, band, :]
                    last, _ = lanes_at(k, step * planes + p)
                    fill = pltpu.roll(fills, lax.rem(128 - last, 128), 1)
                    fill = jnp.concatenate([fill, fill], axis=1)
                    ahead = jnp.where(at_last, fill, pltpu.roll(field, depth - 1, 1))
                    behind = jnp.where(at_first, fill, pltpu.roll(field, 1, 1))
                    return ahead - behind

                one = second_diff(2) - third_diff(1)
                two = third_diff(0) - first_diff(2)
                three = first_diff(1) - second_diff(0)
                mag = jnp.sqrt(1.0 + 0.25 * (one * one + two * two + three * three))
                both.append(mag)
                for t in range(tiles):
                    turned[t, pl.ds(lo * planes + p, tall, stride=planes), :] = mag[
                        :, t * 128 : (t + 1) * 128
                    ]
            if with_level:
                keep_rows(summed, pair * rows + lo, both[0] + both[1])
    if with_level:
        level = pair_lanes(pair_rows(summed, planes // 2 * rows // 2)) * 0.125
        level_out[...] = level.reshape(planes // 2, rows // 2, depth // 2)
    size = each * planes
    mask = rows // each - 1
    for m, out in zip(shifts, mags):
        at = pl.multiple_of(size * jnp.bitwise_and(jnp.bitwise_xor(me, m), mask), size)
        for t in range(tiles):
            for y in range(each):
                out[y, :, t * 128 : (t + 1) * 128] = turned[t, pl.ds(at + y * planes, planes), :]


def curl(velocity, shifts, pos, bands, halos, level=None, with_level=True, n=8):
    _, X, Y, Z = velocity.shape
    H = Y // bands
    each = Y // n
    planes = PLANES
    tiles = Z // 128
    (x_before, x_after), (y_before, y_after), (z_before, z_after) = halos

    def single(comp, shift):
        def index(i, pos):
            at = jnp.minimum(jnp.maximum(i * planes + shift, 0), X - 1)
            return (comp, at, pos[0], 0)

        return pl.BlockSpec((1, 1, H, Z), index)

    def beside(shift):
        def index(i, pos):
            at = pos[0] * (H // 8) + shift
            return (0, i, jnp.minimum(jnp.maximum(at, 0), Y // 8 - 1), 0)

        return pl.BlockSpec((3, planes, 8, Z), index)

    plane_spec = pl.BlockSpec((2, H, Z), lambda i, pos: (0, pos[0], 0))
    row_spec = pl.BlockSpec((2, planes, Z), lambda i, pos: (0, i, 0))
    lane_spec = pl.BlockSpec((H, 128), lambda i, pos: (pos[0], 0))
    in_specs = [
        pl.BlockSpec((3, planes, H, Z), lambda i, pos: (0, i, pos[0], 0)),
        single(1, -1),
        single(1, planes),
        single(2, -1),
        single(2, planes),
        beside(-1),
        beside(H // 8),
        plane_spec,
        plane_spec,
        row_spec,
        row_spec,
        lane_spec,
        lane_spec,
    ]
    args = [velocity] * 7 + [x_before, x_after, y_before, y_after, z_before, z_after]
    aliases = {}
    out_specs = [pl.BlockSpec((each, planes, Z), lambda i, pos: (0, i, 0))] * len(shifts)
    out_shape = [jax.ShapeDtypeStruct((each, X, Z), F32)] * len(shifts)
    scratch = [pltpu.VMEM((tiles, planes * H, 128), F32)]
    if with_level:
        out_specs.append(pl.BlockSpec((planes // 2, H // 2, Z // 2), lambda i, pos: (i, pos[0], 0)))
        out_shape.append(jax.ShapeDtypeStruct((X // 2, Y // 2, Z // 2), F32))
        scratch.append(pltpu.VMEM((tiles, planes // 2 * H, 128), F32))
        if level is not None:
            in_specs.append(pl.BlockSpec(memory_space=pl.ANY))
            args.append(level)
            aliases = {len(args): len(shifts)}
    cells = X * H * Z
    return pl.pallas_call(
        functools.partial(curl_kernel, shifts, each, with_level),
        grid_spec=pltpu.PrefetchScalarGridSpec(
            num_scalar_prefetch=1,
            grid=(X // planes,),
            in_specs=in_specs,
            out_specs=out_specs,
            scratch_shapes=scratch,
        ),
        out_shape=out_shape,
        input_output_aliases=aliases,
        cost_estimate=pl.CostEstimate(
            flops=20 * cells, bytes_accessed=20 * cells, transcendentals=cells
        ),
        name="curl",
    )(pos, *args)


def lay_kernel(shifts, pos, *refs):
    blocks = refs[: len(shifts)]
    out, placed, into, away = refs[-4:]
    depth = blocks[0].shape[2]
    fetches = [
        pltpu.make_async_copy(block, placed.at[k], into.at[k]) for k, block in enumerate(blocks)
    ]
    for fetch in fetches:
        fetch.start()
    copies = []
    for k, m in enumerate(shifts):
        fetches[k].wait()
        at = pl.multiple_of(jnp.bitwise_xor(pos[1], m) * depth, depth)
        copy = pltpu.make_async_copy(placed.at[k], out.at[:, :, pl.ds(at, depth)], away.at[k])
        copy.start()
        copies.append(copy)
    for copy in copies:
        copy.wait()


def lay(blocks, shifts, pos, pencil=None, n=8):
    each, X, Z = blocks[0].shape
    count = len(shifts)
    anywhere = pl.BlockSpec(memory_space=pl.ANY)
    in_specs = [pl.BlockSpec(memory_space=pltpu.SMEM)] + [anywhere] * count
    args = [pos, *blocks]
    aliases = {}
    if pencil is not None:
        in_specs.append(anywhere)
        args.append(pencil)
        aliases = {count + 1: 0}
    return pl.pallas_call(
        functools.partial(lay_kernel, shifts),
        in_specs=in_specs,
        out_specs=anywhere,
        out_shape=jax.ShapeDtypeStruct((each, X, n * Z), F32),
        scratch_shapes=[
            pltpu.VMEM((count, each, X, Z), F32),
            pltpu.SemaphoreType.DMA((count,)),
            pltpu.SemaphoreType.DMA((count,)),
        ],
        input_output_aliases=aliases,
        cost_estimate=pl.CostEstimate(
            flops=count * each * X * Z, bytes_accessed=8 * count * each * X * Z, transcendentals=0
        ),
        name="lay",
    )(*args)


def levels_kernel(pos, *refs):
    blocks = refs[:8]
    one, two, three, four, five, s1, s2, s3, s4 = refs[8:]
    width = blocks[0].shape[2]
    me = pos[1]
    near = jnp.where(me < 4, 4, 2) + jnp.bitwise_and(me, 1)
    far = jnp.where(me < 4, 6, 0) + jnp.bitwise_and(me, 1)
    sources = (me, jnp.bitwise_xor(me, 2), near, far)
    for k, block in enumerate(blocks):
        source = jnp.bitwise_xor(sources[k % 4], k // 4)
        at = pl.multiple_of(source * width, width)
        one[:, :, pl.ds(at, width)] = block[...]

    def up(planes, scratch):
        half, count = len(planes) // 2, planes[0].shape[0]
        for i in range(half):
            keep_rows(scratch, i * count, planes[2 * i] + planes[2 * i + 1])
        result = pair_lanes(pair_rows(scratch, half * count // 2)) * 0.125
        return [result[i * (count // 2) : (i + 1) * (count // 2), :] for i in range(half)]

    planes = up([one[i] for i in range(one.shape[0])], s1)
    for i, plane in enumerate(planes):
        two[i] = plane
    for target, scratch in ((three, s2), (four, s3), (five, s4)):
        planes = up(planes, scratch)
        for i, plane in enumerate(planes):
            for j in range(plane.shape[0]):
                target[j, i : i + 1, :] = plane[j : j + 1, :]


def levels(blocks, pos, n=8):
    planes, rows, width = blocks[0].shape
    depth = width * n
    shapes = [(planes >> k, rows >> k, depth >> k) for k in range(5)]
    outs = shapes[:2] + [(r, p, d) for p, r, d in shapes[2:]]
    vmem = pl.BlockSpec(memory_space=pltpu.VMEM)
    return pl.pallas_call(
        levels_kernel,
        in_specs=[pl.BlockSpec(memory_space=pltpu.SMEM)] + [vmem] * len(blocks),
        out_specs=[vmem] * 5,
        out_shape=[jax.ShapeDtypeStruct(s, F32) for s in outs],
        scratch_shapes=[pltpu.VMEM((s[2] // 128, s[0] // 2 * s[1], 128), F32) for s in shapes[:4]],
        cost_estimate=pl.CostEstimate(
            flops=4 * planes * rows * depth, bytes_accessed=10 * planes * rows * depth, transcendentals=0
        ),
        name="levels",
    )(pos, *blocks)


def send(value, pairs):
    return lax.ppermute(value, "gz", pairs)


def swap(value, m):
    return send(value, [(i, i ^ m) for i in range(lax.axis_size("gz"))])


def chips(value, pairs):
    return send(value, [(2 * a + core, 2 * b + core) for a, b in pairs for core in (0, 1)])


def exchange(first, last, axis):
    peers = lax.axis_size(axis)
    up = [(i, (i + 1) % peers) for i in range(peers)]
    down = [(j, i) for i, j in up]
    return lax.ppermute(last, axis, up), lax.ppermute(first, axis, down)


def on_device(velocity):
    at = lax.axis_index("gz").astype(jnp.int32)
    own = lax.shift_right_logical(at, jnp.int32(2))
    pos_first = jnp.stack([lax.shift_right_logical(at, jnp.int32(1)) ^ 2, at, jnp.int32(4)])
    pos_far = jnp.stack([1 - own, at, jnp.int32(2)])
    pos_near = jnp.stack([own, at, jnp.int32(2)])
    x_first, x_last, y_first, y_last = edges(velocity)
    x_halo = exchange(x_first, x_last, "gx")
    y_halo = exchange(y_first, y_last, "gy")
    lane_first, lane_last = ends(velocity)
    z_halo = exchange(lane_first, lane_last, "gz")
    halos = (x_halo, y_halo, z_halo)
    blocks = {}
    blocks[4], blocks[5] = curl(velocity, (4, 5), pos_first, 4, halos, with_level=False)
    blocks[6], blocks[7], level = curl(velocity, (6, 7), pos_far, 2, halos)
    *near, level = curl(velocity, (0, 1, 2, 3), pos_near, 2, halos, level)
    blocks.update(enumerate(near))
    side = swap(level, 2)
    across = [(1, 2), (2, 1)]
    outward = [(1, 0), (2, 3)]
    close = chips(level, across)
    distant = chips(side, across)
    close_out = chips(close, outward)
    distant_out = chips(distant, outward)
    mine = [level, side, close + close_out, distant + distant_out]
    theirs = [swap(value, 1) for value in mine]
    got = {0: blocks[0]}
    for m in range(1, 8):
        got[m] = swap(blocks[m], m)
    upper = levels([*mine, *theirs], pos_near)
    upper = [*upper[:2]] + [jnp.transpose(value, (1, 0, 2)) for value in upper[2:]]
    pencil = None
    for which in LAYS:
        pencil = lay([got[m] for m in which], which, pos_near, pencil)
    return (jnp.transpose(pencil, (1, 0, 2)), *upper)


LAYS = ((0, 1, 2, 3, 4, 5), (6,), (7,))


def solution(mesh):
    in_specs = (P(None, "gx", "gy", "gz"),)
    out_specs = (
        P("gx", ("gy", "gz"), None),
        P("gx", "gy", None),
        P("gx", "gy", None),
        P("gx", "gy", None),
        P("gx", "gy", None),
        P("gx", "gy", None),
    )

    return jax.shard_map(
        on_device, mesh=mesh, in_specs=in_specs, out_specs=out_specs, check_vma=False
    )
```

time: 132 us -> 148 us (1.12)
  Pallas kernels: 30.1 us -> 40.9 us
  starting transfers between devices: 47.6 us -> 52.9 us
  other arithmetic: 1.18 us -> 3.46 us
  waiting for transfers between devices: 48.7 us -> 46.5 us
    pallas_call x3 -> x5, Pallas kernels: 19.7 us -> 27.9 us  [the longest x3 21.4 us: curl(): pl.pallas_call(functools.partial(curl_kernel, shifts, each, with_level),...]
    ppermute x14 -> x16, starting transfers between devices: 28 us -> 34.4 us  [send(): return lax.ppermute(value, 'gz', pairs)]
    pallas_call x2 -> x3, Pallas kernels: 5.12 us -> 8 us  [lay(): pl.pallas_call(functools.partial(lay_kernel, shifts), in_specs=in_specs,...]
    add x0 -> x2, other arithmetic: none -> 2.22 us  [on_device(): mine = [level, side, close + close_out, distant + distant_out]]
    ppermute x14 -> x16, waiting for transfers between devices: 47.1 us -> 45.1 us  [send(): return lax.ppermute(value, 'gz', pairs)]
    unnamed x32 -> x38, local copies, waits for them, and re-layouts: 2.15 us -> 3.01 us
  transfers between devices with their start and end apart: 20 -> 22, of which waited for: 8 -> 7; matrix products, arithmetic and copies ran while one was open for 1% -> 2% of each run, Pallas kernels for 14% -> 13%
where the time goes in v1:
time: 148 us
  starting transfers between devices  52.9 us (36%)
  waiting for transfers between devices  46.5 us (31%)
  Pallas kernels  40.9 us (28%)
  other arithmetic  3.46 us (2%)
  local copies, waits for them, and re-layouts  3.01 us (2%)
    ppermute x16, waiting for transfers between devices, send(): return lax.ppermute(value, 'gz', pairs)  45.1 us
    ppermute x16, starting transfers between devices, send(): return lax.ppermute(value, 'gz', pairs)  34.4 us
    pallas_call x3, Pallas kernels, curl(): pl.pallas_call(functools.partial(curl_kernel, shifts, each, with_level),...  21.4 us
    ppermute x6, starting transfers between devices, exchange(): return (lax.ppermute(last, axis, up), lax.ppermute(first, axis, down))  18.5 us
    pallas_call x3, Pallas kernels, lay(): pl.pallas_call(functools.partial(lay_kernel, shifts), in_specs=in_specs,...  8 us
    pallas_call x1, Pallas kernels, ends(): pl.pallas_call(ends_kernel, grid=(X // PLANES,), in_specs=[pl.BlockSpec((...  5.01 us
    pallas_call x1, Pallas kernels, levels(): pl.pallas_call(levels_kernel, in_specs=[pl.BlockSpec(memory_space=pltpu.S...  4.31 us
    unnamed x38, local copies, waits for them, and re-layouts  3.01 us
  transfers between devices with their start and end apart: 22, of which 7 were waited for; matrix products, arithmetic and copies ran while one was open for 2% of the time, Pallas kernels for 13%

profile of v1, /device:TPU:1, one launch (start us, length us, event | category | flops | bytes accessed | tf_op | source)
XLA Modules:
  0.0 147.7 jit_solution(11598177385462157750)
XLA Ops:
  0.6 2.2 %edges.1 = (f32[2,96,256]{2,1,0:T(8,128)}, f32[2,96,256]{2,1,0:T(8,128)}, f32[2,32,256]{2,1,0:T(8,128)}, f32[2,32,256]{2,1,0:T(8,128)}) custom-call(f32[3,32,96,256]{3,2,1,0:T(8,128)} %refs_1_.5, f32[3,32,96,256]{3,2,1,0:T(8,128)} %refs_1_.5, f32[3,32,96,256]{3,2,1,0:T(8,128)} %refs_1_.5, f32[3,32,96,256]{3,2,1,0:T(8,128)} %refs_1_.5, ...), custom_call_target="tpu_custom_call" | custom-call | flops 1000000 | bytes 2000000 | tf_op jit(solution)/shard_map/edges/pallas_call | solution.py:67
  2.8 2.0 %collective-permute-start = (f32[2,96,256]{2,1,0:T(8,128)}, f32[2,96,256]{2,1,0:T(8,128)S(1)}, u32[]{:S(2)}, u32[]{:S(2)}) collective-permute-start(f32[2,96,256]{2,1,0:T(8,128)} %get-tuple-element.27), channel_id=1, source_target_pairs={{0,64},{64,128},{128,192},{192,0},{1,65},{65,129},{129,193},{193,1... | collective-permute-start | bytes 589832 | tf_op jit(solution)/shard_map/ppermute | solution.py:392
  4.8 1.3 collective-permute-start.1
  6.2 1.4 collective-permute-start.2
  7.6 8.1 %collective-permute-start.3 = (f32[2,32,256]{2,1,0:T(8,128)}, f32[2,32,256]{2,1,0:T(8,128)S(1)}, u32[]{:S(2)}, u32[]{:S(2)}) collective-permute-start(f32[2,32,256]{2,1,0:T(8,128)} %get-tuple-element.30), channel_id=1, source_target_pairs={{8,0},{16,8},{24,16},{32,24},{40,32},{48,40},{56,48},{0,56},{9,1},... | collective-permute-start | bytes 196616 | tf_op jit(solution)/shard_map/ppermute | solution.py:392
  15.7 5.0 %ends.1 = (f32[96,128]{1,0:T(8,128)}, f32[96,128]{1,0:T(8,128)}) custom-call(f32[3,32,96,256]{3,2,1,0:T(8,128)} %refs_1_.5), custom_call_target="tpu_custom_call" | custom-call | flops 4000000 | bytes 7000000 | tf_op jit(solution)/shard_map/ends/pallas_call | solution.py:107
  20.7 2.1 %collective-permute-start.4 = (f32[96,128]{1,0:T(8,128)}, f32[96,128]{1,0:T(8,128)S(1)}, u32[]{:S(2)}, u32[]{:S(2)}) collective-permute-start(f32[96,128]{1,0:T(8,128)} %get-tuple-element.31), channel_id=1, source_target_pairs={{0,1},{1,2},{2,3},{3,4},{4,5},{5,6},{6,7},{7,0},{8,9},{9,10},{10,1... | collective-permute-start | bytes 147464 | tf_op jit(solution)/shard_map/ppermute | solution.py:392
  22.8 0.7 pad_add_fusion
  23.5 0.8 collective-permute-done.4.refs_6_
  24.3 3.5 %collective-permute-start.5 = (f32[96,128]{1,0:T(8,128)}, f32[96,128]{1,0:T(8,128)S(1)}, u32[]{:S(2)}, u32[]{:S(2)}) collective-permute-start(f32[96,128]{1,0:T(8,128)} %get-tuple-element.32), channel_id=1, source_target_pairs={{1,0},{2,1},{3,2},{4,3},{5,4},{6,5},{7,6},{0,7},{9,8},{10,9},{11,1... | collective-permute-start | bytes 147464 | tf_op jit(solution)/shard_map/ppermute | solution.py:392
  27.8 0.6 pad_add_fusion.1.pos
  28.4 0.5 collective-permute-done.5.refs_7_
  28.9 0.0 collective-permute-done.2.refs_4_
  28.9 0.0 collective-permute-done.3.refs_5_
  28.9 0.0 collective-permute-done.refs_2_
  29.0 0.0 collective-permute-done.1.refs_3_
  29.0 0.5 copy-done.8
  29.5 0.0 copy-done.5
  29.6 0.0 copy-done.6
  29.6 0.1 copy-done
  29.6 0.1 copy-done.1
  29.7 7.8 %curl.3 = (f32[12,32,256]{2,1,0:T(8,128)}, f32[12,32,256]{2,1,0:T(8,128)}, f32[16,48,128]{2,1,0:T(8,128)}) custom-call(s32[3]{0:T(128)} %get-tuple-element.48.pos, f32[3,32,96,256]{3,2,1,0:T(8,128)} %refs_1_.5, f32[3,32,96,256]{3,2,1,0:T(8,128)} %refs_1_.5, f32[3,32,96,256]{3,2,1,0:T(8,128)} %refs_1_.5, f32[3,32,96,256]{3,2,1,0:T(8,128)} %refs_1_.5, ...), custom_call_target="tpu_custom_call" | custom-call | flops 7864320 | bytes 7864320 | tf_op jit(solution)/shard_map/curl/pallas_call | solution.py:260
  37.5 7.9 %curl.4 = (f32[12,32,256]{2,1,0:T(8,128)}, f32[12,32,256]{2,1,0:T(8,128)}, f32[12,32,256]{2,1,0:T(8,128)}, f32[12,32,256]{2,1,0:T(8,128)}, f32[16,48,128]{2,1,0:T(8,128)}) custom-call(s32[3]{0:T(128)} %pad_add_fusion.1.pos, f32[3,32,96,256]{3,2,1,0:T(8,128)} %refs_1_.5, f32[3,32,96,256]{3,2,1,0:T(8,128)} %refs_1_.5, ...), custom_call_target="tpu_custom_call", output_to_operand_aliasing={{4}: (14, {})} | custom-call | flops 7864320 | bytes 7864320 | tf_op jit(solution)/shard_map/curl/pallas_call | solution.py:260
  45.4 0.6 collective-permute-start.13
  46.0 0.7 collective-permute-start.14
  46.7 8.7 %collective-permute-done.13.refs_1_ = f32[16,48,128]{2,1,0:T(8,128)S(1)} collective-permute-done((f32[16,48,128]{2,1,0:T(8,128)}, f32[16,48,128]{2,1,0:T(8,128)S(1)}, u32[]{:S(2)}, u32[]{:S(2)}) %collective-permute-start.13) | collective-permute-done | bytes 393248 | tf_op jit(solution)/shard_map/ppermute | solution.py:377
  55.4 0.7 collective-permute-start.16
  56.1 3.5 %collective-permute-start.7 = (f32[12,32,256]{2,1,0:T(8,128)}, f32[12,32,256]{2,1,0:T(8,128)S(1)}, u32[]{:S(2)}, u32[]{:S(2)}) collective-permute-start(f32[12,32,256]{2,1,0:T(8,128)} %get-tuple-element.34), channel_id=1, source_target_pairs={{0,6},{1,7},{2,4},{3,5},{4,2},{5,3},{6,0},{7,1},{8,14},{9,15},{10,... | collective-permute-start | bytes 1179656 | tf_op jit(solution)/shard_map/ppermute | solution.py:377
  59.6 0.0 collective-permute-done.14
  59.6 1.3 collective-permute-start.15
  60.9 0.0 collective-permute-done.16
  60.9 1.3 collective-permute-start.17
  62.2 0.1 collective-permute-start.8
  62.3 18.3 %collective-permute-start.9 = (f32[12,32,256]{2,1,0:T(8,128)}, f32[12,32,256]{2,1,0:T(8,128)S(1)}, u32[]{:S(2)}, u32[]{:S(2)}) collective-permute-start(f32[12,32,256]{2,1,0:T(8,128)} %get-tuple-element.38), channel_id=1, source_target_pairs={{0,2},{1,3},{2,0},{3,1},{4,6},{5,7},{6,4},{7,5},{8,10},{9,11},{10,... | collective-permute-start | bytes 1179656 | tf_op jit(solution)/shard_map/ppermute | solution.py:377
  80.5 5.7 %curl.5 = (f32[12,32,256]{2,1,0:T(8,128)}, f32[12,32,256]{2,1,0:T(8,128)}) custom-call(s32[3]{0:T(128)} %get-tuple-element.49.pos, f32[3,32,96,256]{3,2,1,0:T(8,128)} %refs_1_.5, f32[3,32,96,256]{3,2,1,0:T(8,128)} %refs_1_.5, f32[3,32,96,256]{3,2,1,0:T(8,128)} %refs_1_.5, f32[3,32,96,256]{3,2,1,0:T(8,128)} %refs_1_.5, f32[3,32,96,256]{3,2,1,0:T(8,128)} %refs_1_.5, ...), custom_call_target="tpu_custom_call" | custom-call | flops 3932160 | bytes 3932160 | tf_op jit(solution)/shard_map/curl/pallas_call | solution.py:260
  86.3 0.0 collective-permute-done.7.refs_0_
  86.3 0.0 copy-start.18
  86.3 1.1 collective-permute-start.10
  87.4 0.0 collective-permute-done.15
  87.4 1.2 collective-permute-start.11
  88.7 0.3 collective-permute-done.17
  89.0 0.8 copy-done.15
  89.7 1.2 collective-permute-start.12
  90.9 1.0 add.6.refs_2_
  92.0 1.2 add.7.refs_3_
  93.1 0.0 collective-permute-done.8.refs_1_
  93.2 0.6 collective-permute-start.18
  93.8 12.6 %collective-permute-done.9.refs_2_ = f32[12,32,256]{2,1,0:T(8,128)S(1)} collective-permute-done((f32[12,32,256]{2,1,0:T(8,128)}, f32[12,32,256]{2,1,0:T(8,128)S(1)}, u32[]{:S(2)}, u32[]{:S(2)}) %collective-permute-start.9) | collective-permute-done | bytes 393248 | tf_op jit(solution)/shard_map/ppermute | solution.py:377
  106.4 3.3 %collective-permute-start.6 = (f32[12,32,256]{2,1,0:T(8,128)}, f32[12,32,256]{2,1,0:T(8,128)}, u32[]{:S(2)}, u32[]{:S(2)}) collective-permute-start(f32[12,32,256]{2,1,0:T(8,128)} %get-tuple-element.33), channel_id=1, source_target_pairs={{0,7},{1,6},{2,5},{3,4},{4,3},{5,2},{6,1},{7,0},{8,15},{9,14},{10,... | collective-permute-start | bytes 1179656 | tf_op jit(solution)/shard_map/ppermute | solution.py:377
  109.8 5.7 %collective-permute-done.10.refs_3_ = f32[12,32,256]{2,1,0:T(8,128)S(1)} collective-permute-done((f32[12,32,256]{2,1,0:T(8,128)}, f32[12,32,256]{2,1,0:T(8,128)S(1)}, u32[]{:S(2)}, u32[]{:S(2)}) %collective-permute-start.10) | collective-permute-done | bytes 393248 | tf_op jit(solution)/shard_map/ppermute | solution.py:377
  115.5 0.0 collective-permute-start.19
  115.5 0.0 collective-permute-done.11.refs_4_
  115.5 0.5 collective-permute-start.20
  116.0 17.7 %collective-permute-done.12.refs_5_ = f32[12,32,256]{2,1,0:T(8,128)S(1)} collective-permute-done((f32[12,32,256]{2,1,0:T(8,128)}, f32[12,32,256]{2,1,0:T(8,128)S(1)}, u32[]{:S(2)}, u32[]{:S(2)}) %collective-permute-start.12) | collective-permute-done | bytes 393248 | tf_op jit(solution)/shard_map/ppermute | solution.py:377
  133.8 0.0 collective-permute-start.21
  133.8 0.7 copy-done.13
  134.5 3.2 %lay.3.refs_1_ = f32[12,32,2048]{2,1,0:T(8,128)} custom-call(s32[3]{0:T(128)} %pad_add_fusion.1.pos, f32[12,32,256]{2,1,0:T(8,128)} %get-tuple-element.36.refs_0_, f32[12,32,256]{2,1,0:T(8,128)} %copy-done.9, f32[12,32,256]{2,1,0:T(8,128)} %copy-done.10, f32[12,32,256]{2,1,0:T(8,128)} %copy-done.11, f32[12,32,256]{2,1,0:T(8,128)} %copy-done.12, ...), custom_call_target="tpu_custom_call" | custom-call | flops 589824 | bytes 4718592 | tf_op jit(solution)/shard_map/lay/pallas_call | solution.py:309
  137.7 2.4 %lay.4.refs_1_ = f32[12,32,2048]{2,1,0:T(8,128)} custom-call(s32[3]{0:T(128)} %pad_add_fusion.1.pos, f32[12,32,256]{2,1,0:T(8,128)} %copy-done.18, f32[12,32,2048]{2,1,0:T(8,128)} %lay.3.refs_1_), custom_call_target="tpu_custom_call", output_to_operand_aliasing={{}: (2, {})} | custom-call | flops 98304 | bytes 786432 | tf_op jit(solution)/shard_map/lay/pallas_call | solution.py:309
  140.1 0.0 collective-permute-done.6.refs_0_
  140.1 2.4 %lay.5 = f32[12,32,2048]{2,1,0:T(8,128)} custom-call(s32[3]{0:T(128)} %pad_add_fusion.1.pos, f32[12,32,256]{2,1,0:T(8,128)} %collective-permute-done.6.refs_0_, f32[12,32,2048]{2,1,0:T(8,128)} %lay.4.refs_1_), custom_call_target="tpu_custom_call", output_to_operand_aliasing={{}: (2, {})} | custom-call | flops 98304 | bytes 786432 | tf_op jit(solution)/shard_map/lay/pallas_call | solution.py:309
  142.6 0.0 collective-permute-done.19.refs_5_
  142.6 0.0 collective-permute-done.20.refs_6_
  142.6 0.7 copy-done.17
  143.4 4.3 %levels.1 = (f32[16,48,1024]{2,1,0:T(8,128)}, f32[8,24,512]{2,1,0:T(8,128)}, f32[12,4,256]{2,1,0:T(4,128)}, f32[6,2,128]{2,1,0:T(2,128)}, f32[3,1,64]{2,1,0:T(1,128)}) custom-call(s32[3]{0:T(128)} %pad_add_fusion.1.pos, f32[16,48,128]{2,1,0:T(8,128)} %get-tuple-element.42.refs_0_, f32[16,48,128]{2,1,0:T(8,128)} %copy-done.16, f32[16,48,128]{2,1,0:T(8,128)} %copy-done.3, ...), custom_call_target="tpu_custom_call" | custom-call | flops 3145728 | bytes 7864320 | tf_op jit(solution)/shard_map/levels/pallas_call | solution.py:363
  (31 shorter events, 0.1 us)
Async XLA Ops:
  2.8 26.1 %collective-permute-start = (f32[2,96,256]{2,1,0:T(8,128)}, f32[2,96,256]{2,1,0:T(8,128)S(1)}, u32[]{:S(2)}, u32[]{:S(2)}) collective-permute-start(f32[2,96,256]{2,1,0:T(8,128)} %get-tuple-element.27), channel_id=1, source_target_pairs={{0,64},{64,128},{128,192},{192,0},{1,65},{65,129},{129,193},{193,1... | collective-permute-start | bytes 589832 | tf_op jit(solution)/shard_map/ppermute | solution.py:392
  4.8 24.1 %collective-permute-start.1 = (f32[2,96,256]{2,1,0:T(8,128)}, f32[2,96,256]{2,1,0:T(8,128)S(1)}, u32[]{:S(2)}, u32[]{:S(2)}) collective-permute-start(f32[2,96,256]{2,1,0:T(8,128)} %get-tuple-element.28), channel_id=1, source_target_pairs={{64,0},{128,64},{192,128},{0,192},{65,1},{129,65},{193,129},{1,193... | collective-permute-start | bytes 589832 | tf_op jit(solution)/shard_map/ppermute | solution.py:392
  6.2 22.7 %collective-permute-start.2 = (f32[2,32,256]{2,1,0:T(8,128)}, f32[2,32,256]{2,1,0:T(8,128)S(1)}, u32[]{:S(2)}, u32[]{:S(2)}) collective-permute-start(f32[2,32,256]{2,1,0:T(8,128)} %get-tuple-element.29), channel_id=1, source_target_pairs={{0,8},{8,16},{16,24},{24,32},{32,40},{40,48},{48,56},{56,0},{1,9},... | collective-permute-start | bytes 196616 | tf_op jit(solution)/shard_map/ppermute | solution.py:392
  7.6 21.3 %collective-permute-start.3 = (f32[2,32,256]{2,1,0:T(8,128)}, f32[2,32,256]{2,1,0:T(8,128)S(1)}, u32[]{:S(2)}, u32[]{:S(2)}) collective-permute-start(f32[2,32,256]{2,1,0:T(8,128)} %get-tuple-element.30), channel_id=1, source_target_pairs={{8,0},{16,8},{24,16},{32,24},{40,32},{48,40},{56,48},{0,56},{9,1},... | collective-permute-start | bytes 196616 | tf_op jit(solution)/shard_map/ppermute | solution.py:392
  20.7 3.6 %collective-permute-start.4 = (f32[96,128]{1,0:T(8,128)}, f32[96,128]{1,0:T(8,128)S(1)}, u32[]{:S(2)}, u32[]{:S(2)}) collective-permute-start(f32[96,128]{1,0:T(8,128)} %get-tuple-element.31), channel_id=1, source_target_pairs={{0,1},{1,2},{2,3},{3,4},{4,5},{5,6},{6,7},{7,0},{8,9},{9,10},{10,1... | collective-permute-start | bytes 147464 | tf_op jit(solution)/shard_map/ppermute | solution.py:392
  24.3 4.7 %copy-start.7 = (f32[96,128]{1,0:T(8,128)}, f32[96,128]{1,0:T(8,128)S(1)}, u32[]{:S(2)}) copy-start(f32[96,128]{1,0:T(8,128)S(1)} %collective-permute-done.4.refs_6_) | copy-start | bytes 147460
  24.3 4.6 %collective-permute-start.5 = (f32[96,128]{1,0:T(8,128)}, f32[96,128]{1,0:T(8,128)S(1)}, u32[]{:S(2)}, u32[]{:S(2)}) collective-permute-start(f32[96,128]{1,0:T(8,128)} %get-tuple-element.32), channel_id=1, source_target_pairs={{1,0},{2,1},{3,2},{4,3},{5,4},{6,5},{7,6},{0,7},{9,8},{10,9},{11,1... | collective-permute-start | bytes 147464 | tf_op jit(solution)/shard_map/ppermute | solution.py:392
  28.9 0.6 copy-start.8
  28.9 0.6 copy-start.5
  28.9 0.6 copy-start.6
  29.0 0.7 copy-start
  29.0 0.7 copy-start.1
  45.4 10.0 %collective-permute-start.13 = (f32[16,48,128]{2,1,0:T(8,128)}, f32[16,48,128]{2,1,0:T(8,128)S(1)}, u32[]{:S(2)}, u32[]{:S(2)}) collective-permute-start(f32[16,48,128]{2,1,0:T(8,128)} %get-tuple-element.42.refs_0_), channel_id=1, source_target_pairs={{0,2},{1,3},{2,0},{3,1},{4,6},{5,7},{6,4},{7,5},{8,10},{9,11},{10,... | collective-permute-start | bytes 1179656 | tf_op jit(solution)/shard_map/ppermute | solution.py:377
  46.0 13.6 %collective-permute-start.14 = (f32[16,48,128]{2,1,0:T(8,128)}, f32[16,48,128]{2,1,0:T(8,128)S(1)}, u32[]{:S(2)}, u32[]{:S(2)}) collective-permute-start(f32[16,48,128]{2,1,0:T(8,128)} %get-tuple-element.42.refs_0_), channel_id=1, source_target_pairs={{2,4},{3,5},{4,2},{5,3},{10,12},{11,13},{12,10},{13,11},{18,20},{1... | collective-permute-start | bytes 1179656 | tf_op jit(solution)/shard_map/ppermute | solution.py:377
  55.4 30.9 %copy-start.16 = (f32[16,48,128]{2,1,0:T(8,128)}, f32[16,48,128]{2,1,0:T(8,128)S(1)}, u32[]{:S(2)}) copy-start(f32[16,48,128]{2,1,0:T(8,128)S(1)} %collective-permute-done.13.refs_1_) | copy-start | bytes 1179652
  55.4 5.5 %collective-permute-start.16 = (f32[16,48,128]{2,1,0:T(8,128)S(1)}, f32[16,48,128]{2,1,0:T(8,128)S(1)}, u32[]{:S(2)}, u32[]{:S(2)}) collective-permute-start(f32[16,48,128]{2,1,0:T(8,128)S(1)} %collective-permute-done.13.refs_1_), channel_id=1, source_target_pairs={{2,4},{3,5},{4,2},{5,3},{10,12},{11,13},{12,10},{13,11},{18,20},{1... | collective-permute-start | bytes 1179656 | tf_op jit(solution)/shard_map/ppermute | solution.py:377
  56.1 30.2 %collective-permute-start.7 = (f32[12,32,256]{2,1,0:T(8,128)}, f32[12,32,256]{2,1,0:T(8,128)S(1)}, u32[]{:S(2)}, u32[]{:S(2)}) collective-permute-start(f32[12,32,256]{2,1,0:T(8,128)} %get-tuple-element.34), channel_id=1, source_target_pairs={{0,6},{1,7},{2,4},{3,5},{4,2},{5,3},{6,0},{7,1},{8,14},{9,15},{10,... | collective-permute-start | bytes 1179656 | tf_op jit(solution)/shard_map/ppermute | solution.py:377
  59.6 27.8 %collective-permute-start.15 = (f32[16,48,128]{2,1,0:T(8,128)S(1)}, f32[16,48,128]{2,1,0:T(8,128)S(1)}, u32[]{:S(2)}, u32[]{:S(2)}) collective-permute-start(f32[16,48,128]{2,1,0:T(8,128)S(1)} %collective-permute-done.14), channel_id=1, source_target_pairs={{2,0},{3,1},{4,6},{5,7},{10,8},{11,9},{12,14},{13,15},{18,16},{19,... | collective-permute-start | bytes 1179656 | tf_op jit(solution)/shard_map/ppermute | solution.py:377
  60.9 28.1 %collective-permute-start.17 = (f32[16,48,128]{2,1,0:T(8,128)S(1)}, f32[16,48,128]{2,1,0:T(8,128)S(1)}, u32[]{:S(2)}, u32[]{:S(2)}) collective-permute-start(f32[16,48,128]{2,1,0:T(8,128)S(1)} %collective-permute-done.16), channel_id=1, source_target_pairs={{2,0},{3,1},{4,6},{5,7},{10,8},{11,9},{12,14},{13,15},{18,16},{19,... | collective-permute-start | bytes 1179656 | tf_op jit(solution)/shard_map/ppermute | solution.py:377
  62.2 31.0 %collective-permute-start.8 = (f32[12,32,256]{2,1,0:T(8,128)}, f32[12,32,256]{2,1,0:T(8,128)S(1)}, u32[]{:S(2)}, u32[]{:S(2)}) collective-permute-start(f32[12,32,256]{2,1,0:T(8,128)} %get-tuple-element.37), channel_id=1, source_target_pairs={{0,1},{1,0},{2,3},{3,2},{4,5},{5,4},{6,7},{7,6},{8,9},{9,8},{10,11... | collective-permute-start | bytes 1179656 | tf_op jit(solution)/shard_map/ppermute | solution.py:377
  62.3 44.2 %collective-permute-start.9 = (f32[12,32,256]{2,1,0:T(8,128)}, f32[12,32,256]{2,1,0:T(8,128)S(1)}, u32[]{:S(2)}, u32[]{:S(2)}) collective-permute-start(f32[12,32,256]{2,1,0:T(8,128)} %get-tuple-element.38), channel_id=1, source_target_pairs={{0,2},{1,3},{2,0},{3,1},{4,6},{5,7},{6,4},{7,5},{8,10},{9,11},{10,... | collective-permute-start | bytes 1179656 | tf_op jit(solution)/shard_map/ppermute | solution.py:377
  80.5 12.6 %copy-start.2 = (f32[16,48,128]{2,1,0:T(8,128)S(1)}, f32[16,48,128]{2,1,0:T(8,128)}, u32[]{:S(2)}) copy-start(f32[16,48,128]{2,1,0:T(8,128)} %get-tuple-element.42.refs_0_) | copy-start | bytes 1179652
  86.3 1.2 copy-start.18
  86.3 29.2 %collective-permute-start.10 = (f32[12,32,256]{2,1,0:T(8,128)}, f32[12,32,256]{2,1,0:T(8,128)S(1)}, u32[]{:S(2)}, u32[]{:S(2)}) collective-permute-start(f32[12,32,256]{2,1,0:T(8,128)} %get-tuple-element.39), channel_id=1, source_target_pairs={{0,3},{1,2},{2,1},{3,0},{4,7},{5,6},{6,5},{7,4},{8,11},{9,10},{10,... | collective-permute-start | bytes 1179656 | tf_op jit(solution)/shard_map/ppermute | solution.py:377
  87.4 2.3 %copy-start.14 = (f32[16,48,128]{2,1,0:T(8,128)}, f32[16,48,128]{2,1,0:T(8,128)S(1)}, u32[]{:S(2)}) copy-start(f32[16,48,128]{2,1,0:T(8,128)S(1)} %collective-permute-done.15) | copy-start | bytes 1179652
  87.4 28.1 %collective-permute-start.11 = (f32[12,32,256]{2,1,0:T(8,128)}, f32[12,32,256]{2,1,0:T(8,128)S(1)}, u32[]{:S(2)}, u32[]{:S(2)}) collective-permute-start(f32[12,32,256]{2,1,0:T(8,128)} %get-tuple-element.40), channel_id=1, source_target_pairs={{0,4},{1,5},{2,6},{3,7},{4,0},{5,1},{6,2},{7,3},{8,12},{9,13},{10,... | collective-permute-start | bytes 1179656 | tf_op jit(solution)/shard_map/ppermute | solution.py:377
  89.0 0.8 copy-start.15
  89.7 44.0 %collective-permute-start.12 = (f32[12,32,256]{2,1,0:T(8,128)}, f32[12,32,256]{2,1,0:T(8,128)S(1)}, u32[]{:S(2)}, u32[]{:S(2)}) collective-permute-start(f32[12,32,256]{2,1,0:T(8,128)} %get-tuple-element.41), channel_id=1, source_target_pairs={{0,5},{1,4},{2,7},{3,6},{4,1},{5,0},{6,3},{7,2},{8,13},{9,12},{10,... | collective-permute-start | bytes 1179656 | tf_op jit(solution)/shard_map/ppermute | solution.py:377
  91.9 45.7 %copy-start.3 = (f32[16,48,128]{2,1,0:T(8,128)}, f32[16,48,128]{2,1,0:T(8,128)S(1)}, u32[]{:S(2)}) copy-start(f32[16,48,128]{2,1,0:T(8,128)S(1)} %add.6.refs_2_) | copy-start | bytes 1179652
  93.1 47.0 %copy-start.4 = (f32[16,48,128]{2,1,0:T(8,128)}, f32[16,48,128]{2,1,0:T(8,128)S(1)}, u32[]{:S(2)}) copy-start(f32[16,48,128]{2,1,0:T(8,128)S(1)} %add.7.refs_3_) | copy-start | bytes 1179652
  93.2 40.6 %copy-start.9 = (f32[12,32,256]{2,1,0:T(8,128)}, f32[12,32,256]{2,1,0:T(8,128)S(1)}, u32[]{:S(2)}) copy-start(f32[12,32,256]{2,1,0:T(8,128)S(1)} %collective-permute-done.8.refs_1_) | copy-start | bytes 1179652
  93.2 49.4 %collective-permute-start.18 = (f32[16,48,128]{2,1,0:T(8,128)S(1)}, f32[16,48,128]{2,1,0:T(8,128)S(1)}, u32[]{:S(2)}, u32[]{:S(2)}) collective-permute-start(f32[16,48,128]{2,1,0:T(8,128)S(1)} %copy-done.2), channel_id=1, source_target_pairs={{0,1},{1,0},{2,3},{3,2},{4,5},{5,4},{6,7},{7,6},{8,9},{9,8},{10,11... | collective-permute-start | bytes 1179656 | tf_op jit(solution)/shard_map/ppermute | solution.py:377
  106.4 27.3 %copy-start.10 = (f32[12,32,256]{2,1,0:T(8,128)}, f32[12,32,256]{2,1,0:T(8,128)S(1)}, u32[]{:S(2)}) copy-start(f32[12,32,256]{2,1,0:T(8,128)S(1)} %collective-permute-done.9.refs_2_) | copy-start | bytes 1179652
  106.4 33.7 %collective-permute-start.6 = (f32[12,32,256]{2,1,0:T(8,128)}, f32[12,32,256]{2,1,0:T(8,128)}, u32[]{:S(2)}, u32[]{:S(2)}) collective-permute-start(f32[12,32,256]{2,1,0:T(8,128)} %get-tuple-element.33), channel_id=1, source_target_pairs={{0,7},{1,6},{2,5},{3,4},{4,3},{5,2},{6,1},{7,0},{8,15},{9,14},{10,... | collective-permute-start | bytes 1179656 | tf_op jit(solution)/shard_map/ppermute | solution.py:377
  115.5 18.3 %copy-start.11 = (f32[12,32,256]{2,1,0:T(8,128)}, f32[12,32,256]{2,1,0:T(8,128)S(1)}, u32[]{:S(2)}) copy-start(f32[12,32,256]{2,1,0:T(8,128)S(1)} %collective-permute-done.10.refs_3_) | copy-start | bytes 1179652
  115.5 27.1 %collective-permute-start.19 = (f32[16,48,128]{2,1,0:T(8,128)}, f32[16,48,128]{2,1,0:T(8,128)}, u32[]{:S(2)}, u32[]{:S(2)}) collective-permute-start(f32[16,48,128]{2,1,0:T(8,128)} %copy-done.16), channel_id=1, source_target_pairs={{0,1},{1,0},{2,3},{3,2},{4,5},{5,4},{6,7},{7,6},{8,9},{9,8},{10,11... | collective-permute-start | bytes 1179656 | tf_op jit(solution)/shard_map/ppermute | solution.py:377
  115.5 18.3 %copy-start.12 = (f32[12,32,256]{2,1,0:T(8,128)}, f32[12,32,256]{2,1,0:T(8,128)S(1)}, u32[]{:S(2)}) copy-start(f32[12,32,256]{2,1,0:T(8,128)S(1)} %collective-permute-done.11.refs_4_) | copy-start | bytes 1179652
  115.5 27.1 %collective-permute-start.20 = (f32[16,48,128]{2,1,0:T(8,128)S(1)}, f32[16,48,128]{2,1,0:T(8,128)}, u32[]{:S(2)}, u32[]{:S(2)}) collective-permute-start(f32[16,48,128]{2,1,0:T(8,128)S(1)} %add.6.refs_2_), channel_id=1, source_target_pairs={{0,1},{1,0},{2,3},{3,2},{4,5},{5,4},{6,7},{7,6},{8,9},{9,8},{10,11... | collective-permute-start | bytes 1179656 | tf_op jit(solution)/shard_map/ppermute | solution.py:377
  133.7 0.8 copy-start.13
  133.8 8.9 %collective-permute-start.21 = (f32[16,48,128]{2,1,0:T(8,128)S(1)}, f32[16,48,128]{2,1,0:T(8,128)}, u32[]{:S(2)}, u32[]{:S(2)}) collective-permute-start(f32[16,48,128]{2,1,0:T(8,128)S(1)} %add.7.refs_3_), channel_id=1, source_target_pairs={{0,1},{1,0},{2,3},{3,2},{4,5},{5,4},{6,7},{7,6},{8,9},{9,8},{10,11... | collective-permute-start | bytes 1179656 | tf_op jit(solution)/shard_map/ppermute | solution.py:377
  142.6 0.8 copy-start.17

commit v2 on v1

--- a/solution.py
+++ b/solution.py
@@ -43,79 +43,79 @@
     return parts[0] if len(parts) == 1 else jnp.concatenate(parts, axis=1)
 
 
-def edges_kernel(v0, v1, w0, w1, ut, ub, wt, wb, x_first, x_last, y_first, y_last):
-    for k, (first, last) in enumerate(((v0, v1), (w0, w1))):
-        x_first[k] = first[0, 0]
-        x_last[k] = last[0, 0]
-    for k, (top, bottom) in enumerate(((ut, ub), (wt, wb))):
-        for p in range(top.shape[1]):
-            y_first[k, p : p + 1, :] = top[0, p, 0:1, :]
-            y_last[k, p : p + 1, :] = bottom[0, p, 7:8, :]
-
-
-def edges(velocity):
-    _, X, Y, Z = velocity.shape
-
-    def plane(comp, at):
-        return pl.BlockSpec((1, 1, Y, Z), lambda i: (comp, at, 0, 0))
-
-    def rows(comp, at):
-        return pl.BlockSpec((1, X, 8, Z), lambda i: (comp, 0, at, 0))
-
-    planes = jax.ShapeDtypeStruct((2, Y, Z), F32)
-    lines = jax.ShapeDtypeStruct((2, X, Z), F32)
-    return pl.pallas_call(
-        edges_kernel,
-        grid=(1,),
-        in_specs=[plane(1, 0), plane(1, X - 1), plane(2, 0), plane(2, X - 1)]
-        + [rows(0, 0), rows(0, Y // 8 - 1), rows(2, 0), rows(2, Y // 8 - 1)],
-        out_specs=[pl.BlockSpec(s.shape, lambda i: (0, 0, 0)) for s in (planes, planes, lines, lines)],
-        out_shape=[planes, planes, lines, lines],
-        cost_estimate=pl.CostEstimate(flops=1_000_000, bytes_accessed=2_000_000, transcendentals=0),
-        name="edges",
-    )(*[velocity] * 8)
-
-
 def lanes_at(k, x):
     last = 2 * (k * 32 + x)
     return last, lax.rem(last + 127, 128)
 
 
-def ends_kernel(vel, lane_first, lane_last):
-    step = pl.program_id(0)
-    _, planes, rows, depth = vel.shape
+def ends_kernel(
+    velocity, x_first, x_last, y_first, y_last, z_first, z_last, uv, w_planes, w_rows, sems
+):
+    _, X, rows, depth = velocity.shape
+    chunk = 4
+    chunks = X // chunk
+    pieces = [
+        (velocity.at[0:2, c * chunk : (c + 1) * chunk], uv.at[:, c * chunk : (c + 1) * chunk])
+        for c in range(chunks)
+    ]
+    pieces += [(velocity.at[2, at], w_planes.at[i]) for i, at in enumerate((0, X - 1))]
+    pieces += [
+        (velocity.at[2, :, at : at + 8, :], w_rows.at[i]) for i, at in enumerate((0, rows - 8))
+    ]
+    copies = [pltpu.make_async_copy(a, b, sems.at[i]) for i, (a, b) in enumerate(pieces)]
+    for copy in copies:
+        copy.start()
     lane = lax.broadcasted_iota(jnp.int32, (rows, 128), 1)
-    first = lane_first[...]
-    last = lane_last[...]
-    for k in range(2):
-        for p in range(planes):
-            to_last, to_first = lanes_at(k, step * planes + p)
-            first = jnp.where(
-                lane == to_first, pltpu.roll(vel[k, p, :, :128], to_first, 1), first
-            )
-            last = jnp.where(
-                lane == to_last, pltpu.roll(vel[k, p, :, depth - 128 :], to_last + 1, 1), last
-            )
-    lane_first[...] = first
-    lane_last[...] = last
+    first = jnp.zeros((rows, 128), F32)
+    last = jnp.zeros((rows, 128), F32)
+    for c in range(chunks):
+        copies[c].wait()
+        for p in range(c * chunk, (c + 1) * chunk):
+            for k in range(2):
+                to_last = 2 * (k * 32 + p)
+                to_first = (to_last + 127) % 128
+                first = jnp.where(
+                    lane == to_first, pltpu.roll(uv[k, p, :, :128], to_first, 1), first
+                )
+                last = jnp.where(
+                    lane == to_last,
+                    pltpu.roll(uv[k, p, :, depth - 128 :], (to_last + 1) % 128, 1),
+                    last,
+                )
+            y_first[0, p : p + 1, :] = uv[0, p, 0:1, :]
+            y_last[0, p : p + 1, :] = uv[0, p, rows - 1 : rows, :]
+    z_first[...] = first
+    z_last[...] = last
+    for copy in copies[chunks:]:
+        copy.wait()
+    for i, (out, at) in enumerate(((x_first, 0), (x_last, X - 1))):
+        out[0] = uv[1, at]
+        out[1] = w_planes[i]
+    for p in range(X):
+        y_first[1, p : p + 1, :] = w_rows[0, p, 0:1, :]
+        y_last[1, p : p + 1, :] = w_rows[1, p, 7:8, :]
 
 
 def ends(velocity):
     _, X, Y, Z = velocity.shape
-    lanes = jax.ShapeDtypeStruct((Y, 128), F32)
-    spec = pl.BlockSpec((Y, 128), lambda i: (0, 0))
+    outs = [jax.ShapeDtypeStruct(s, F32) for s in ((2, Y, Z), (2, X, Z), (Y, 128)) for _ in range(2)]
     return pl.pallas_call(
         ends_kernel,
-        grid=(X // PLANES,),
-        in_specs=[pl.BlockSpec((2, PLANES, Y, Z), lambda i: (0, i, 0, 0))],
-        out_specs=[spec, spec],
-        out_shape=[lanes, lanes],
-        cost_estimate=pl.CostEstimate(flops=4_000_000, bytes_accessed=7_000_000, transcendentals=0),
+        in_specs=[pl.BlockSpec(memory_space=pl.ANY)],
+        out_specs=[pl.BlockSpec(memory_space=pltpu.VMEM)] * 6,
+        out_shape=outs,
+        scratch_shapes=[
+            pltpu.VMEM((2, X, Y, Z), F32),
+            pltpu.VMEM((2, Y, Z), F32),
+            pltpu.VMEM((2, X, 8, Z), F32),
+            pltpu.SemaphoreType.DMA((X // 4 + 4,)),
+        ],
+        cost_estimate=pl.CostEstimate(flops=4_000_000, bytes_accessed=8_000_000, transcendentals=0),
         name="ends",
     )(velocity)
 
 
-def curl_kernel(shifts, each, with_level, pos, vel, v_before, v_after, w_before, w_after, *refs):
+def curl_kernel(shifts, each, with_level, which, bands, pos, vel, v_before, v_after, w_before, w_after, *refs):
     above, below, x_before, x_after, y_before, y_after, z_before, z_after = refs[:8]
     count = len(shifts)
     if with_level:
@@ -124,7 +124,7 @@
     else:
         turned = refs[-1]
         mags = refs[-1 - count : -1]
-    band_at, me, bands = pos[0], pos[1], pos[2]
+    band_at, me = pos[which], pos[0]
     step = pl.program_id(0)
     _, planes, rows, depth = vel.shape
     tall = 2 * each
@@ -203,7 +203,7 @@
                 out[y, :, t * 128 : (t + 1) * 128] = turned[t, pl.ds(at + y * planes, planes), :]
 
 
-def curl(velocity, shifts, pos, bands, halos, level=None, with_level=True, n=8):
+def curl(velocity, shifts, pos, which, bands, halos, level=None, with_level=True, n=8):
     _, X, Y, Z = velocity.shape
     H = Y // bands
     each = Y // n
@@ -214,22 +214,22 @@
     def single(comp, shift):
         def index(i, pos):
             at = jnp.minimum(jnp.maximum(i * planes + shift, 0), X - 1)
-            return (comp, at, pos[0], 0)
+            return (comp, at, pos[which], 0)
 
         return pl.BlockSpec((1, 1, H, Z), index)
 
     def beside(shift):
         def index(i, pos):
-            at = pos[0] * (H // 8) + shift
+            at = pos[which] * (H // 8) + shift
             return (0, i, jnp.minimum(jnp.maximum(at, 0), Y // 8 - 1), 0)
 
         return pl.BlockSpec((3, planes, 8, Z), index)
 
-    plane_spec = pl.BlockSpec((2, H, Z), lambda i, pos: (0, pos[0], 0))
+    plane_spec = pl.BlockSpec((2, H, Z), lambda i, pos: (0, pos[which], 0))
     row_spec = pl.BlockSpec((2, planes, Z), lambda i, pos: (0, i, 0))
-    lane_spec = pl.BlockSpec((H, 128), lambda i, pos: (pos[0], 0))
+    lane_spec = pl.BlockSpec((H, 128), lambda i, pos: (pos[which], 0))
     in_specs = [
-        pl.BlockSpec((3, planes, H, Z), lambda i, pos: (0, i, pos[0], 0)),
+        pl.BlockSpec((3, planes, H, Z), lambda i, pos: (0, i, pos[which], 0)),
         single(1, -1),
         single(1, planes),
         single(2, -1),
@@ -249,7 +249,7 @@
     out_shape = [jax.ShapeDtypeStruct((each, X, Z), F32)] * len(shifts)
     scratch = [pltpu.VMEM((tiles, planes * H, 128), F32)]
     if with_level:
-        out_specs.append(pl.BlockSpec((planes // 2, H // 2, Z // 2), lambda i, pos: (i, pos[0], 0)))
+        out_specs.append(pl.BlockSpec((planes // 2, H // 2, Z // 2), lambda i, pos: (i, pos[which], 0)))
         out_shape.append(jax.ShapeDtypeStruct((X // 2, Y // 2, Z // 2), F32))
         scratch.append(pltpu.VMEM((tiles, planes // 2 * H, 128), F32))
         if level is not None:
@@ -258,7 +258,7 @@
             aliases = {len(args): len(shifts)}
     cells = X * H * Z
     return pl.pallas_call(
-        functools.partial(curl_kernel, shifts, each, with_level),
+        functools.partial(curl_kernel, shifts, each, with_level, which, bands),
         grid_spec=pltpu.PrefetchScalarGridSpec(
             num_scalar_prefetch=1,
             grid=(X // planes,),
@@ -277,20 +277,14 @@
 
 def lay_kernel(shifts, pos, *refs):
     blocks = refs[: len(shifts)]
-    out, placed, into, away = refs[-4:]
+    out, away = refs[-2:]
     depth = blocks[0].shape[2]
-    fetches = [
-        pltpu.make_async_copy(block, placed.at[k], into.at[k]) for k, block in enumerate(blocks)
-    ]
-    for fetch in fetches:
-        fetch.start()
     copies = []
-    for k, m in enumerate(shifts):
-        fetches[k].wait()
-        at = pl.multiple_of(jnp.bitwise_xor(pos[1], m) * depth, depth)
-        copy = pltpu.make_async_copy(placed.at[k], out.at[:, :, pl.ds(at, depth)], away.at[k])
+    for k, (m, block) in enumerate(zip(shifts, blocks)):
+        at = pl.multiple_of(jnp.bitwise_xor(pos[0], m) * depth, depth)
+        copies.append(pltpu.make_async_copy(block, out.at[:, :, pl.ds(at, depth)], away.at[k]))
+    for copy in copies:
         copy.start()
-        copies.append(copy)
     for copy in copies:
         copy.wait()
 
@@ -311,11 +305,8 @@
         in_specs=in_specs,
         out_specs=anywhere,
         out_shape=jax.ShapeDtypeStruct((each, X, n * Z), F32),
-        scratch_shapes=[
-            pltpu.VMEM((count, each, X, Z), F32),
-            pltpu.SemaphoreType.DMA((count,)),
-            pltpu.SemaphoreType.DMA((count,)),
-        ],
+        scratch_shapes=[pltpu.SemaphoreType.DMA((count,))],
+        compiler_params=pltpu.CompilerParams(vmem_limit_bytes=1 << 20),
         input_output_aliases=aliases,
         cost_estimate=pl.CostEstimate(
             flops=count * each * X * Z, bytes_accessed=8 * count * each * X * Z, transcendentals=0
@@ -328,7 +319,7 @@
     blocks = refs[:8]
     one, two, three, four, five, s1, s2, s3, s4 = refs[8:]
     width = blocks[0].shape[2]
-    me = pos[1]
+    me = pos[0]
     near = jnp.where(me < 4, 4, 2) + jnp.bitwise_and(me, 1)
     far = jnp.where(me < 4, 6, 0) + jnp.bitwise_and(me, 1)
     sources = (me, jnp.bitwise_xor(me, 2), near, far)
@@ -369,6 +360,7 @@
         cost_estimate=pl.CostEstimate(
             flops=4 * planes * rows * depth, bytes_accessed=10 * planes * rows * depth, transcendentals=0
         ),
+        compiler_params=pltpu.CompilerParams(vmem_limit_bytes=24 << 20),
         name="levels",
     )(pos, *blocks)
 
@@ -395,19 +387,16 @@
 def on_device(velocity):
     at = lax.axis_index("gz").astype(jnp.int32)
     own = lax.shift_right_logical(at, jnp.int32(2))
-    pos_first = jnp.stack([lax.shift_right_logical(at, jnp.int32(1)) ^ 2, at, jnp.int32(4)])
-    pos_far = jnp.stack([1 - own, at, jnp.int32(2)])
-    pos_near = jnp.stack([own, at, jnp.int32(2)])
-    x_first, x_last, y_first, y_last = edges(velocity)
+    pos = jnp.stack([at, lax.shift_right_logical(at, jnp.int32(1)) ^ 2, 1 - own, own])
+    x_first, x_last, y_first, y_last, z_first, z_last = ends(velocity)
+    y_halo = exchange(y_first, y_last, "gy")
     x_halo = exchange(x_first, x_last, "gx")
-    y_halo = exchange(y_first, y_last, "gy")
-    lane_first, lane_last = ends(velocity)
-    z_halo = exchange(lane_first, lane_last, "gz")
+    z_halo = exchange(z_first, z_last, "gz")
     halos = (x_halo, y_halo, z_halo)
     blocks = {}
-    blocks[4], blocks[5] = curl(velocity, (4, 5), pos_first, 4, halos, with_level=False)
-    blocks[6], blocks[7], level = curl(velocity, (6, 7), pos_far, 2, halos)
-    *near, level = curl(velocity, (0, 1, 2, 3), pos_near, 2, halos, level)
+    blocks[4], blocks[5] = curl(velocity, (4, 5), pos, 1, 4, halos, with_level=False)
+    blocks[6], blocks[7], level = curl(velocity, (6, 7), pos, 2, 2, halos)
+    *near, level = curl(velocity, (0, 1, 2, 3), pos, 3, 2, halos, level)
     blocks.update(enumerate(near))
     side = swap(level, 2)
     across = [(1, 2), (2, 1)]
@@ -421,15 +410,15 @@
     got = {0: blocks[0]}
     for m in range(1, 8):
         got[m] = swap(blocks[m], m)
-    upper = levels([*mine, *theirs], pos_near)
+    upper = levels([*mine, *theirs], pos)
     upper = [*upper[:2]] + [jnp.transpose(value, (1, 0, 2)) for value in upper[2:]]
     pencil = None
     for which in LAYS:
-        pencil = lay([got[m] for m in which], which, pos_near, pencil)
+        pencil = lay([got[m] for m in which], which, pos, pencil)
     return (jnp.transpose(pencil, (1, 0, 2)), *upper)
 
 
-LAYS = ((0, 1, 2, 3, 4, 5), (6,), (7,))
+LAYS = ((0, 1, 3, 4, 5), (2, 6), (7,))
 
 
 def solution(mesh):

time: 148 us -> 141 us (0.953)
  the two profiles are of different devices: /device:TPU:1 before, /device:TPU:57 now
where the time goes in v2:
time: 141 us
  starting transfers between devices  64.4 us (46%)
  waiting for transfers between devices  39.3 us (28%)
  Pallas kernels  33.1 us (23%)
  other arithmetic  1.75 us (1%)
    ppermute x16, starting transfers between devices, send(): return lax.ppermute(value, 'gz', pairs)  54 us
    ppermute x16, waiting for transfers between devices, send(): return lax.ppermute(value, 'gz', pairs)  29.9 us
    pallas_call x3, Pallas kernels, curl(): pl.pallas_call(functools.partial(curl_kernel, shifts, each, with_level, w...  21.2 us
    ppermute x6, starting transfers between devices, exchange(): return (lax.ppermute(last, axis, up), lax.ppermute(first, axis, down))  10.4 us
    ppermute x6, waiting for transfers between devices, exchange(): return (lax.ppermute(last, axis, up), lax.ppermute(first, axis, down))  9.48 us
    pallas_call x3, Pallas kernels, lay(): pl.pallas_call(functools.partial(lay_kernel, shifts), in_specs=in_specs,...  4.59 us
    pallas_call x1, Pallas kernels, ends(): pl.pallas_call(ends_kernel, in_specs=[pl.BlockSpec(memory_space=pl.ANY)],...  4.27 us
    pallas_call x1, Pallas kernels, levels(): pl.pallas_call(levels_kernel, in_specs=[pl.BlockSpec(memory_space=pltpu.S...  3.02 us
  transfers between devices with their start and end apart: 22, of which 9 were waited for; matrix products, arithmetic and copies ran while one was open for 1% of the time, Pallas kernels for 7%

profile of v2, /device:TPU:57, one launch (start us, length us, event | category | flops | bytes accessed | tf_op | source)
XLA Modules:
  0.0 140.8 jit_solution(10764300367709845717)
XLA Ops:
  0.6 4.3 %ends.1 = (f32[2,96,256]{2,1,0:T(8,128)}, f32[2,96,256]{2,1,0:T(8,128)}, f32[2,32,256]{2,1,0:T(8,128)}, f32[2,32,256]{2,1,0:T(8,128)}, f32[96,128]{1,0:T(8,128)}, /*index=5*/f32[96,128]{1,0:T(8,128)}) custom-call(f32[3,32,96,256]{3,2,1,0:T(8,128)} %refs_1_.5), custom_call_target="tpu_custom_call" | custom-call | flops 4000000 | bytes 8000000 | tf_op jit(solution)/shard_map/ends/pallas_call | solution.py:102
  4.9 1.3 collective-permute-start
  6.2 1.5 %collective-permute-start.1 = (f32[2,96,256]{2,1,0:T(8,128)}, f32[2,96,256]{2,1,0:T(8,128)S(1)}, u32[]{:S(2)}, u32[]{:S(2)}) collective-permute-start(f32[2,96,256]{2,1,0:T(8,128)} %get-tuple-element.28), channel_id=1, source_target_pairs={{64,0},{128,64},{192,128},{0,192},{65,1},{129,65},{193,129},{1,193... | collective-permute-start | bytes 589832 | tf_op jit(solution)/shard_map/ppermute | solution.py:384
  7.7 2.8 %collective-permute-start.4 = (f32[96,128]{1,0:T(8,128)}, f32[96,128]{1,0:T(8,128)S(1)}, u32[]{:S(2)}, u32[]{:S(2)}) collective-permute-start(f32[96,128]{1,0:T(8,128)} %get-tuple-element.31), channel_id=1, source_target_pairs={{0,1},{1,2},{2,3},{3,4},{4,5},{5,6},{6,7},{7,0},{8,9},{9,10},{10,1... | collective-permute-start | bytes 147464 | tf_op jit(solution)/shard_map/ppermute | solution.py:384
  10.4 4.8 %collective-permute-start.2 = (f32[2,32,256]{2,1,0:T(8,128)}, f32[2,32,256]{2,1,0:T(8,128)S(1)}, u32[]{:S(2)}, u32[]{:S(2)}) collective-permute-start(f32[2,32,256]{2,1,0:T(8,128)} %get-tuple-element.29), channel_id=1, source_target_pairs={{0,8},{8,16},{16,24},{24,32},{32,40},{40,48},{48,56},{56,0},{1,9},... | collective-permute-start | bytes 196616 | tf_op jit(solution)/shard_map/ppermute | solution.py:384
  15.2 0.0 collective-permute-start.3
  15.2 0.0 collective-permute-done.4.refs_6_
  15.2 0.0 copy-start.7
  15.2 0.1 collective-permute-start.5
  15.3 0.7 pad_add_fusion.pos
  16.0 3.7 %collective-permute-done.5.refs_7_ = f32[96,128]{1,0:T(8,128)S(1)} collective-permute-done((f32[96,128]{1,0:T(8,128)}, f32[96,128]{1,0:T(8,128)S(1)}, u32[]{:S(2)}, u32[]{:S(2)}) %collective-permute-start.5) | collective-permute-done | bytes 49184 | tf_op jit(solution)/shard_map/ppermute | solution.py:384
  19.7 0.0 collective-permute-done.2.refs_4_
  19.7 5.8 %collective-permute-done.3.refs_5_ = f32[2,32,256]{2,1,0:T(8,128)S(1)} collective-permute-done((f32[2,32,256]{2,1,0:T(8,128)}, f32[2,32,256]{2,1,0:T(8,128)S(1)}, u32[]{:S(2)}, u32[]{:S(2)}) %collective-permute-start.3) | collective-permute-done | bytes 65568 | tf_op jit(solution)/shard_map/ppermute | solution.py:384
  25.4 0.0 collective-permute-done.refs_2_
  25.4 0.0 collective-permute-done.1.refs_3_
  25.4 0.0 copy-done.7
  25.5 0.0 copy-done.8
  25.5 0.0 copy-done.5
  25.5 0.6 copy-done.6
  26.1 0.1 copy-done.3
  26.1 0.7 copy-done.4
  26.8 7.8 %curl.3 = (f32[12,32,256]{2,1,0:T(8,128)}, f32[12,32,256]{2,1,0:T(8,128)}, f32[16,48,128]{2,1,0:T(8,128)}) custom-call(s32[4]{0:T(128)} %pad_add_fusion.pos, f32[3,32,96,256]{3,2,1,0:T(8,128)} %refs_1_.5, f32[3,32,96,256]{3,2,1,0:T(8,128)} %refs_1_.5, f32[3,32,96,256]{3,2,1,0:T(8,128)} %refs_1_.5, f32[3,32,96,256]{3,2,1,0:T(8,128)} %refs_1_.5, ...), custom_call_target="tpu_custom_call" | custom-call | flops 7864320 | bytes 7864320 | tf_op jit(solution)/shard_map/curl/pallas_call | solution.py:260
  34.6 7.9 %curl.4 = (f32[12,32,256]{2,1,0:T(8,128)}, f32[12,32,256]{2,1,0:T(8,128)}, f32[12,32,256]{2,1,0:T(8,128)}, f32[12,32,256]{2,1,0:T(8,128)}, f32[16,48,128]{2,1,0:T(8,128)}) custom-call(s32[4]{0:T(128)} %pad_add_fusion.pos, f32[3,32,96,256]{3,2,1,0:T(8,128)} %refs_1_.5, f32[3,32,96,256]{3,2,1,0:T(8,128)} %refs_1_.5, ...), custom_call_target="tpu_custom_call", output_to_operand_aliasing={{4}: (14, {})} | custom-call | flops 7864320 | bytes 7864320 | tf_op jit(solution)/shard_map/curl/pallas_call | solution.py:260
  42.5 0.9 collective-permute-start.13
  43.4 3.2 %collective-permute-start.14 = (f32[16,48,128]{2,1,0:T(8,128)}, f32[16,48,128]{2,1,0:T(8,128)S(1)}, u32[]{:S(2)}, u32[]{:S(2)}) collective-permute-start(f32[16,48,128]{2,1,0:T(8,128)} %get-tuple-element.42.refs_0_), channel_id=1, source_target_pairs={{2,4},{3,5},{4,2},{5,3},{10,12},{11,13},{12,10},{13,11},{18,20},{1... | collective-permute-start | bytes 1179656 | tf_op jit(solution)/shard_map/ppermute | solution.py:369
  46.6 6.3 %collective-permute-done.13.refs_1_ = f32[16,48,128]{2,1,0:T(8,128)S(1)} collective-permute-done((f32[16,48,128]{2,1,0:T(8,128)}, f32[16,48,128]{2,1,0:T(8,128)S(1)}, u32[]{:S(2)}, u32[]{:S(2)}) %collective-permute-start.13) | collective-permute-done | bytes 393248 | tf_op jit(solution)/shard_map/ppermute | solution.py:369
  52.9 4.0 %collective-permute-start.16 = (f32[16,48,128]{2,1,0:T(8,128)S(1)}, f32[16,48,128]{2,1,0:T(8,128)S(1)}, u32[]{:S(2)}, u32[]{:S(2)}) collective-permute-start(f32[16,48,128]{2,1,0:T(8,128)S(1)} %collective-permute-done.13.refs_1_), channel_id=1, source_target_pairs={{2,4},{3,5},{4,2},{5,3},{10,12},{11,13},{12,10},{13,11},{18,20},{1... | collective-permute-start | bytes 1179656 | tf_op jit(solution)/shard_map/ppermute | solution.py:369
  57.0 0.1 collective-permute-start.7
  57.1 0.0 collective-permute-done.14
  57.1 3.4 %collective-permute-start.15 = (f32[16,48,128]{2,1,0:T(8,128)S(1)}, f32[16,48,128]{2,1,0:T(8,128)S(1)}, u32[]{:S(2)}, u32[]{:S(2)}) collective-permute-start(f32[16,48,128]{2,1,0:T(8,128)S(1)} %collective-permute-done.14), channel_id=1, source_target_pairs={{2,0},{3,1},{4,6},{5,7},{10,8},{11,9},{12,14},{13,15},{18,16},{19,... | collective-permute-start | bytes 1179656 | tf_op jit(solution)/shard_map/ppermute | solution.py:369
  60.5 4.6 %collective-permute-done.16 = f32[16,48,128]{2,1,0:T(8,128)S(1)} collective-permute-done((f32[16,48,128]{2,1,0:T(8,128)S(1)}, f32[16,48,128]{2,1,0:T(8,128)S(1)}, u32[]{:S(2)}, u32[]{:S(2)}) %collective-permute-start.16) | collective-permute-done | bytes 393248 | tf_op jit(solution)/shard_map/ppermute | solution.py:369
  65.1 2.0 %collective-permute-start.17 = (f32[16,48,128]{2,1,0:T(8,128)S(1)}, f32[16,48,128]{2,1,0:T(8,128)}, u32[]{:S(2)}, u32[]{:S(2)}) collective-permute-start(f32[16,48,128]{2,1,0:T(8,128)S(1)} %collective-permute-done.16), channel_id=1, source_target_pairs={{2,0},{3,1},{4,6},{5,7},{10,8},{11,9},{12,14},{13,15},{18,16},{19,... | collective-permute-start | bytes 1179656 | tf_op jit(solution)/shard_map/ppermute | solution.py:369
  67.1 1.2 collective-permute-start.8
  68.3 3.1 %collective-permute-start.9 = (f32[12,32,256]{2,1,0:T(8,128)}, f32[12,32,256]{2,1,0:T(8,128)S(1)}, u32[]{:S(2)}, u32[]{:S(2)}) collective-permute-start(f32[12,32,256]{2,1,0:T(8,128)} %get-tuple-element.38), channel_id=1, source_target_pairs={{0,1},{1,0},{2,3},{3,2},{4,5},{5,4},{6,7},{7,6},{8,9},{9,8},{10,11... | collective-permute-start | bytes 1179656 | tf_op jit(solution)/shard_map/ppermute | solution.py:369
  71.4 5.5 %curl.5 = (f32[12,32,256]{2,1,0:T(8,128)}, f32[12,32,256]{2,1,0:T(8,128)}) custom-call(s32[4]{0:T(128)} %pad_add_fusion.pos, f32[3,32,96,256]{3,2,1,0:T(8,128)} %refs_1_.5, f32[3,32,96,256]{3,2,1,0:T(8,128)} %refs_1_.5, f32[3,32,96,256]{3,2,1,0:T(8,128)} %refs_1_.5, f32[3,32,96,256]{3,2,1,0:T(8,128)} %refs_1_.5, f32[3,32,96,256]{3,2,1,0:T(8,128)} %refs_1_.5, ...), custom_call_target="tpu_custom_call" | custom-call | flops 3932160 | bytes 3932160 | tf_op jit(solution)/shard_map/curl/pallas_call | solution.py:260
  77.0 0.0 collective-permute-done.7.refs_0_
  77.0 2.0 %collective-permute-start.10 = (f32[12,32,256]{2,1,0:T(8,128)}, f32[12,32,256]{2,1,0:T(8,128)S(1)}, u32[]{:S(2)}, u32[]{:S(2)}) collective-permute-start(f32[12,32,256]{2,1,0:T(8,128)} %get-tuple-element.39), channel_id=1, source_target_pairs={{0,3},{1,2},{2,1},{3,0},{4,7},{5,6},{6,5},{7,4},{8,11},{9,10},{10,... | collective-permute-start | bytes 1179656 | tf_op jit(solution)/shard_map/ppermute | solution.py:369
  78.9 2.3 %collective-permute-done.15 = f32[16,48,128]{2,1,0:T(8,128)S(1)} collective-permute-done((f32[16,48,128]{2,1,0:T(8,128)S(1)}, f32[16,48,128]{2,1,0:T(8,128)S(1)}, u32[]{:S(2)}, u32[]{:S(2)}) %collective-permute-start.15) | collective-permute-done | bytes 393248 | tf_op jit(solution)/shard_map/ppermute | solution.py:369
  81.2 2.2 %collective-permute-start.11 = (f32[12,32,256]{2,1,0:T(8,128)}, f32[12,32,256]{2,1,0:T(8,128)S(1)}, u32[]{:S(2)}, u32[]{:S(2)}) collective-permute-start(f32[12,32,256]{2,1,0:T(8,128)} %get-tuple-element.40), channel_id=1, source_target_pairs={{0,4},{1,5},{2,6},{3,7},{4,0},{5,1},{6,2},{7,3},{8,12},{9,13},{10,... | collective-permute-start | bytes 1179656 | tf_op jit(solution)/shard_map/ppermute | solution.py:369
  83.5 8.2 %collective-permute-done.17 = f32[16,48,128]{2,1,0:T(8,128)} collective-permute-done((f32[16,48,128]{2,1,0:T(8,128)S(1)}, f32[16,48,128]{2,1,0:T(8,128)}, u32[]{:S(2)}, u32[]{:S(2)}) %collective-permute-start.17) | collective-permute-done | bytes 393248 | tf_op jit(solution)/shard_map/ppermute | solution.py:369
  91.7 7.0 %collective-permute-start.12 = (f32[12,32,256]{2,1,0:T(8,128)}, f32[12,32,256]{2,1,0:T(8,128)S(1)}, u32[]{:S(2)}, u32[]{:S(2)}) collective-permute-start(f32[12,32,256]{2,1,0:T(8,128)} %get-tuple-element.41), channel_id=1, source_target_pairs={{0,5},{1,4},{2,7},{3,6},{4,1},{5,0},{6,3},{7,2},{8,13},{9,12},{10,... | collective-permute-start | bytes 1179656 | tf_op jit(solution)/shard_map/ppermute | solution.py:369
  98.7 1.1 add.7.refs_3_
  99.8 0.0 collective-permute-done.8.refs_1_
  99.8 0.0 copy-done
  99.8 0.1 collective-permute-start.18
  99.9 0.0 collective-permute-done.9.refs_1_
  99.9 0.8 collective-permute-start.6
  100.7 2.4 %collective-permute-done.10.refs_2_ = f32[12,32,256]{2,1,0:T(8,128)S(1)} collective-permute-done((f32[12,32,256]{2,1,0:T(8,128)}, f32[12,32,256]{2,1,0:T(8,128)S(1)}, u32[]{:S(2)}, u32[]{:S(2)}) %collective-permute-start.10) | collective-permute-done | bytes 393248 | tf_op jit(solution)/shard_map/ppermute | solution.py:369
  103.1 2.2 %collective-permute-start.19 = (f32[16,48,128]{2,1,0:T(8,128)S(1)}, f32[16,48,128]{2,1,0:T(8,128)S(1)}, u32[]{:S(2)}, u32[]{:S(2)}) collective-permute-start(f32[16,48,128]{2,1,0:T(8,128)S(1)} %collective-permute-done.13.refs_1_), channel_id=1, source_target_pairs={{0,1},{1,0},{2,3},{3,2},{4,5},{5,4},{6,7},{7,6},{8,9},{9,8},{10,11... | collective-permute-start | bytes 1179656 | tf_op jit(solution)/shard_map/ppermute | solution.py:369
  105.3 0.0 collective-permute-done.11.refs_3_
  105.3 15.9 %collective-permute-start.20 = (f32[16,48,128]{2,1,0:T(8,128)S(1)}, f32[16,48,128]{2,1,0:T(8,128)S(1)}, u32[]{:S(2)}, u32[]{:S(2)}) collective-permute-start(f32[16,48,128]{2,1,0:T(8,128)S(1)} %add.6.refs_2_), channel_id=1, source_target_pairs={{0,1},{1,0},{2,3},{3,2},{4,5},{5,4},{6,7},{7,6},{8,9},{9,8},{10,11... | collective-permute-start | bytes 1179656 | tf_op jit(solution)/shard_map/ppermute | solution.py:369
  121.2 2.5 %collective-permute-done.12.refs_4_ = f32[12,32,256]{2,1,0:T(8,128)S(1)} collective-permute-done((f32[12,32,256]{2,1,0:T(8,128)}, f32[12,32,256]{2,1,0:T(8,128)S(1)}, u32[]{:S(2)}, u32[]{:S(2)}) %collective-permute-start.12) | collective-permute-done | bytes 393248 | tf_op jit(solution)/shard_map/ppermute | solution.py:369
  123.7 5.9 %collective-permute-start.21 = (f32[16,48,128]{2,1,0:T(8,128)S(1)}, f32[16,48,128]{2,1,0:T(8,128)S(1)}, u32[]{:S(2)}, u32[]{:S(2)}) collective-permute-start(f32[16,48,128]{2,1,0:T(8,128)S(1)} %add.7.refs_3_), channel_id=1, source_target_pairs={{0,1},{1,0},{2,3},{3,2},{4,5},{5,4},{6,7},{7,6},{8,9},{9,8},{10,11... | collective-permute-start | bytes 1179656 | tf_op jit(solution)/shard_map/ppermute | solution.py:369
  129.7 0.0 copy-done.1
  129.7 0.0 copy-done.2
  129.7 1.8 %lay.3.refs_2_ = f32[12,32,2048]{2,1,0:T(8,128)} custom-call(s32[4]{0:T(128)S(1)} %copy-done.2, f32[12,32,256]{2,1,0:T(8,128)S(1)} %copy-done.1, f32[12,32,256]{2,1,0:T(8,128)S(1)} %collective-permute-done.9.refs_1_, f32[12,32,256]{2,1,0:T(8,128)S(1)} %collective-permute-done.10.refs_2_, f32[12,32,256]{2,1,0:T(8,128)S(1)} %collective-permute-done.11.refs_3_, ...), custom_call_target="tpu_custom_call" | custom-call | flops 491520 | bytes 3932160 | tf_op jit(solution)/shard_map/lay/pallas_call | solution.py:303
  131.5 1.4 %lay.4.refs_1_ = f32[12,32,2048]{2,1,0:T(8,128)} custom-call(s32[4]{0:T(128)S(1)} %copy-done.2, f32[12,32,256]{2,1,0:T(8,128)S(1)} %collective-permute-done.7.refs_0_, f32[12,32,256]{2,1,0:T(8,128)S(1)} %collective-permute-done.8.refs_1_, f32[12,32,2048]{2,1,0:T(8,128)} %lay.3.refs_2_), custom_call_target="tpu_custom_call", output_to_operand_aliasing={{}: (3, {})} | custom-call | flops 196608 | bytes 1572864 | tf_op jit(solution)/shard_map/lay/pallas_call | solution.py:303
  133.0 3.5 %collective-permute-done.6.refs_0_ = f32[12,32,256]{2,1,0:T(8,128)S(1)} collective-permute-done((f32[12,32,256]{2,1,0:T(8,128)}, f32[12,32,256]{2,1,0:T(8,128)S(1)}, u32[]{:S(2)}, u32[]{:S(2)}) %collective-permute-start.6) | collective-permute-done | bytes 393248 | tf_op jit(solution)/shard_map/ppermute | solution.py:369
  136.4 1.3 lay.5
  137.7 0.0 collective-permute-done.18.refs_4_
  137.8 0.0 collective-permute-done.19.refs_5_
  137.8 0.0 collective-permute-done.20.refs_6_
  137.8 0.0 collective-permute-done.21.refs_7_
  137.8 3.0 %levels.1 = (f32[16,48,1024]{2,1,0:T(8,128)}, f32[8,24,512]{2,1,0:T(8,128)}, f32[12,4,256]{2,1,0:T(4,128)}, f32[6,2,128]{2,1,0:T(2,128)}, f32[3,1,64]{2,1,0:T(1,128)}) custom-call(s32[4]{0:T(128)S(1)} %copy-done.2, f32[16,48,128]{2,1,0:T(8,128)S(1)} %copy-done, f32[16,48,128]{2,1,0:T(8,128)S(1)} %collective-permute-done.13.refs_1_, ...), custom_call_target="tpu_custom_call" | custom-call | flops 3145728 | bytes 7864320 | tf_op jit(solution)/shard_map/levels/pallas_call | solution.py:354
  (9 shorter events, 0.1 us)
Async XLA Ops:
  4.9 20.5 %collective-permute-start = (f32[2,96,256]{2,1,0:T(8,128)}, f32[2,96,256]{2,1,0:T(8,128)S(1)}, u32[]{:S(2)}, u32[]{:S(2)}) collective-permute-start(f32[2,96,256]{2,1,0:T(8,128)} %get-tuple-element.27), channel_id=1, source_target_pairs={{0,64},{64,128},{128,192},{192,0},{1,65},{65,129},{129,193},{193,1... | collective-permute-start | bytes 589832 | tf_op jit(solution)/shard_map/ppermute | solution.py:384
  6.2 19.2 %collective-permute-start.1 = (f32[2,96,256]{2,1,0:T(8,128)}, f32[2,96,256]{2,1,0:T(8,128)S(1)}, u32[]{:S(2)}, u32[]{:S(2)}) collective-permute-start(f32[2,96,256]{2,1,0:T(8,128)} %get-tuple-element.28), channel_id=1, source_target_pairs={{64,0},{128,64},{192,128},{0,192},{65,1},{129,65},{193,129},{1,193... | collective-permute-start | bytes 589832 | tf_op jit(solution)/shard_map/ppermute | solution.py:384
  7.7 7.5 %collective-permute-start.4 = (f32[96,128]{1,0:T(8,128)}, f32[96,128]{1,0:T(8,128)S(1)}, u32[]{:S(2)}, u32[]{:S(2)}) collective-permute-start(f32[96,128]{1,0:T(8,128)} %get-tuple-element.31), channel_id=1, source_target_pairs={{0,1},{1,2},{2,3},{3,4},{4,5},{5,6},{6,7},{7,0},{8,9},{9,10},{10,1... | collective-permute-start | bytes 147464 | tf_op jit(solution)/shard_map/ppermute | solution.py:384
  10.4 9.2 %collective-permute-start.2 = (f32[2,32,256]{2,1,0:T(8,128)}, f32[2,32,256]{2,1,0:T(8,128)S(1)}, u32[]{:S(2)}, u32[]{:S(2)}) collective-permute-start(f32[2,32,256]{2,1,0:T(8,128)} %get-tuple-element.29), channel_id=1, source_target_pairs={{0,8},{8,16},{16,24},{24,32},{32,40},{40,48},{48,56},{56,0},{1,9},... | collective-permute-start | bytes 196616 | tf_op jit(solution)/shard_map/ppermute | solution.py:384
  15.2 10.2 %collective-permute-start.3 = (f32[2,32,256]{2,1,0:T(8,128)}, f32[2,32,256]{2,1,0:T(8,128)S(1)}, u32[]{:S(2)}, u32[]{:S(2)}) collective-permute-start(f32[2,32,256]{2,1,0:T(8,128)} %get-tuple-element.30), channel_id=1, source_target_pairs={{8,0},{16,8},{24,16},{32,24},{40,32},{48,40},{56,48},{0,56},{9,1},... | collective-permute-start | bytes 196616 | tf_op jit(solution)/shard_map/ppermute | solution.py:384
  15.2 10.3 %copy-start.7 = (f32[96,128]{1,0:T(8,128)}, f32[96,128]{1,0:T(8,128)S(1)}, u32[]{:S(2)}) copy-start(f32[96,128]{1,0:T(8,128)S(1)} %collective-permute-done.4.refs_6_) | copy-start | bytes 147460
  15.2 4.4 %collective-permute-start.5 = (f32[96,128]{1,0:T(8,128)}, f32[96,128]{1,0:T(8,128)S(1)}, u32[]{:S(2)}, u32[]{:S(2)}) collective-permute-start(f32[96,128]{1,0:T(8,128)} %get-tuple-element.32), channel_id=1, source_target_pairs={{1,0},{2,1},{3,2},{4,3},{5,4},{6,5},{7,6},{0,7},{9,8},{10,9},{11,1... | collective-permute-start | bytes 147464 | tf_op jit(solution)/shard_map/ppermute | solution.py:384
  19.7 5.8 %copy-start.8 = (f32[96,128]{1,0:T(8,128)}, f32[96,128]{1,0:T(8,128)S(1)}, u32[]{:S(2)}) copy-start(f32[96,128]{1,0:T(8,128)S(1)} %collective-permute-done.5.refs_7_) | copy-start | bytes 147460
  19.7 5.8 %copy-start.5 = (f32[2,32,256]{2,1,0:T(8,128)}, f32[2,32,256]{2,1,0:T(8,128)S(1)}, u32[]{:S(2)}) copy-start(f32[2,32,256]{2,1,0:T(8,128)S(1)} %collective-permute-done.2.refs_4_) | copy-start | bytes 196612
  25.4 0.6 copy-start.6
  25.4 0.7 copy-start.3
  26.1 0.7 copy-start.4
  42.5 10.4 %collective-permute-start.13 = (f32[16,48,128]{2,1,0:T(8,128)}, f32[16,48,128]{2,1,0:T(8,128)S(1)}, u32[]{:S(2)}, u32[]{:S(2)}) collective-permute-start(f32[16,48,128]{2,1,0:T(8,128)} %get-tuple-element.42.refs_0_), channel_id=1, source_target_pairs={{0,2},{1,3},{2,0},{3,1},{4,6},{5,7},{6,4},{7,5},{8,10},{9,11},{10,... | collective-permute-start | bytes 1179656 | tf_op jit(solution)/shard_map/ppermute | solution.py:369
  43.4 13.7 %collective-permute-start.14 = (f32[16,48,128]{2,1,0:T(8,128)}, f32[16,48,128]{2,1,0:T(8,128)S(1)}, u32[]{:S(2)}, u32[]{:S(2)}) collective-permute-start(f32[16,48,128]{2,1,0:T(8,128)} %get-tuple-element.42.refs_0_), channel_id=1, source_target_pairs={{2,4},{3,5},{4,2},{5,3},{10,12},{11,13},{12,10},{13,11},{18,20},{1... | collective-permute-start | bytes 1179656 | tf_op jit(solution)/shard_map/ppermute | solution.py:369
  52.9 12.2 %collective-permute-start.16 = (f32[16,48,128]{2,1,0:T(8,128)S(1)}, f32[16,48,128]{2,1,0:T(8,128)S(1)}, u32[]{:S(2)}, u32[]{:S(2)}) collective-permute-start(f32[16,48,128]{2,1,0:T(8,128)S(1)} %collective-permute-done.13.refs_1_), channel_id=1, source_target_pairs={{2,4},{3,5},{4,2},{5,3},{10,12},{11,13},{12,10},{13,11},{18,20},{1... | collective-permute-start | bytes 1179656 | tf_op jit(solution)/shard_map/ppermute | solution.py:369
  57.0 20.0 %collective-permute-start.7 = (f32[12,32,256]{2,1,0:T(8,128)}, f32[12,32,256]{2,1,0:T(8,128)S(1)}, u32[]{:S(2)}, u32[]{:S(2)}) collective-permute-start(f32[12,32,256]{2,1,0:T(8,128)} %get-tuple-element.35), channel_id=1, source_target_pairs={{0,2},{1,3},{2,0},{3,1},{4,6},{5,7},{6,4},{7,5},{8,10},{9,11},{10,... | collective-permute-start | bytes 1179656 | tf_op jit(solution)/shard_map/ppermute | solution.py:369
  57.1 24.2 %collective-permute-start.15 = (f32[16,48,128]{2,1,0:T(8,128)S(1)}, f32[16,48,128]{2,1,0:T(8,128)S(1)}, u32[]{:S(2)}, u32[]{:S(2)}) collective-permute-start(f32[16,48,128]{2,1,0:T(8,128)S(1)} %collective-permute-done.14), channel_id=1, source_target_pairs={{2,0},{3,1},{4,6},{5,7},{10,8},{11,9},{12,14},{13,15},{18,16},{19,... | collective-permute-start | bytes 1179656 | tf_op jit(solution)/shard_map/ppermute | solution.py:369
  65.1 26.6 %collective-permute-start.17 = (f32[16,48,128]{2,1,0:T(8,128)S(1)}, f32[16,48,128]{2,1,0:T(8,128)}, u32[]{:S(2)}, u32[]{:S(2)}) collective-permute-start(f32[16,48,128]{2,1,0:T(8,128)S(1)} %collective-permute-done.16), channel_id=1, source_target_pairs={{2,0},{3,1},{4,6},{5,7},{10,8},{11,9},{12,14},{13,15},{18,16},{19,... | collective-permute-start | bytes 1179656 | tf_op jit(solution)/shard_map/ppermute | solution.py:369
  67.1 32.6 %collective-permute-start.8 = (f32[12,32,256]{2,1,0:T(8,128)}, f32[12,32,256]{2,1,0:T(8,128)S(1)}, u32[]{:S(2)}, u32[]{:S(2)}) collective-permute-start(f32[12,32,256]{2,1,0:T(8,128)} %get-tuple-element.36), channel_id=1, source_target_pairs={{0,6},{1,7},{2,4},{3,5},{4,2},{5,3},{6,0},{7,1},{8,14},{9,15},{10,... | collective-permute-start | bytes 1179656 | tf_op jit(solution)/shard_map/ppermute | solution.py:369
  68.3 31.5 %copy-start = (f32[16,48,128]{2,1,0:T(8,128)S(1)}, f32[16,48,128]{2,1,0:T(8,128)}, u32[]{:S(2)}) copy-start(f32[16,48,128]{2,1,0:T(8,128)} %get-tuple-element.42.refs_0_) | copy-start | bytes 1179652
  68.3 61.3 %copy-start.1 = (f32[12,32,256]{2,1,0:T(8,128)S(1)}, f32[12,32,256]{2,1,0:T(8,128)}, u32[]{:S(2)}) copy-start(f32[12,32,256]{2,1,0:T(8,128)} %get-tuple-element.37.refs_0_) | copy-start | bytes 1179652
  68.3 61.3 %copy-start.2 = (s32[4]{0:T(128)S(1)}, s32[4]{0:T(128)}, u32[]{:S(2)}) copy-start(s32[4]{0:T(128)} %pad_add_fusion.pos) | copy-start | bytes 52
  68.3 31.6 %collective-permute-start.9 = (f32[12,32,256]{2,1,0:T(8,128)}, f32[12,32,256]{2,1,0:T(8,128)S(1)}, u32[]{:S(2)}, u32[]{:S(2)}) collective-permute-start(f32[12,32,256]{2,1,0:T(8,128)} %get-tuple-element.38), channel_id=1, source_target_pairs={{0,1},{1,0},{2,3},{3,2},{4,5},{5,4},{6,7},{7,6},{8,9},{9,8},{10,11... | collective-permute-start | bytes 1179656 | tf_op jit(solution)/shard_map/ppermute | solution.py:369
  77.0 26.1 %collective-permute-start.10 = (f32[12,32,256]{2,1,0:T(8,128)}, f32[12,32,256]{2,1,0:T(8,128)S(1)}, u32[]{:S(2)}, u32[]{:S(2)}) collective-permute-start(f32[12,32,256]{2,1,0:T(8,128)} %get-tuple-element.39), channel_id=1, source_target_pairs={{0,3},{1,2},{2,1},{3,0},{4,7},{5,6},{6,5},{7,4},{8,11},{9,10},{10,... | collective-permute-start | bytes 1179656 | tf_op jit(solution)/shard_map/ppermute | solution.py:369
  81.2 24.1 %collective-permute-start.11 = (f32[12,32,256]{2,1,0:T(8,128)}, f32[12,32,256]{2,1,0:T(8,128)S(1)}, u32[]{:S(2)}, u32[]{:S(2)}) collective-permute-start(f32[12,32,256]{2,1,0:T(8,128)} %get-tuple-element.40), channel_id=1, source_target_pairs={{0,4},{1,5},{2,6},{3,7},{4,0},{5,1},{6,2},{7,3},{8,12},{9,13},{10,... | collective-permute-start | bytes 1179656 | tf_op jit(solution)/shard_map/ppermute | solution.py:369
  91.7 32.1 %collective-permute-start.12 = (f32[12,32,256]{2,1,0:T(8,128)}, f32[12,32,256]{2,1,0:T(8,128)S(1)}, u32[]{:S(2)}, u32[]{:S(2)}) collective-permute-start(f32[12,32,256]{2,1,0:T(8,128)} %get-tuple-element.41), channel_id=1, source_target_pairs={{0,5},{1,4},{2,7},{3,6},{4,1},{5,0},{6,3},{7,2},{8,13},{9,12},{10,... | collective-permute-start | bytes 1179656 | tf_op jit(solution)/shard_map/ppermute | solution.py:369
  99.8 38.0 %collective-permute-start.18 = (f32[16,48,128]{2,1,0:T(8,128)S(1)}, f32[16,48,128]{2,1,0:T(8,128)S(1)}, u32[]{:S(2)}, u32[]{:S(2)}) collective-permute-start(f32[16,48,128]{2,1,0:T(8,128)S(1)} %copy-done), channel_id=1, source_target_pairs={{0,1},{1,0},{2,3},{3,2},{4,5},{5,4},{6,7},{7,6},{8,9},{9,8},{10,11... | collective-permute-start | bytes 1179656 | tf_op jit(solution)/shard_map/ppermute | solution.py:369
  99.9 36.5 %collective-permute-start.6 = (f32[12,32,256]{2,1,0:T(8,128)}, f32[12,32,256]{2,1,0:T(8,128)S(1)}, u32[]{:S(2)}, u32[]{:S(2)}) collective-permute-start(f32[12,32,256]{2,1,0:T(8,128)} %get-tuple-element.33), channel_id=1, source_target_pairs={{0,7},{1,6},{2,5},{3,4},{4,3},{5,2},{6,1},{7,0},{8,15},{9,14},{10,... | collective-permute-start | bytes 1179656 | tf_op jit(solution)/shard_map/ppermute | solution.py:369
  103.1 34.6 %collective-permute-start.19 = (f32[16,48,128]{2,1,0:T(8,128)S(1)}, f32[16,48,128]{2,1,0:T(8,128)S(1)}, u32[]{:S(2)}, u32[]{:S(2)}) collective-permute-start(f32[16,48,128]{2,1,0:T(8,128)S(1)} %collective-permute-done.13.refs_1_), channel_id=1, source_target_pairs={{0,1},{1,0},{2,3},{3,2},{4,5},{5,4},{6,7},{7,6},{8,9},{9,8},{10,11... | collective-permute-start | bytes 1179656 | tf_op jit(solution)/shard_map/ppermute | solution.py:369
  105.3 32.4 %collective-permute-start.20 = (f32[16,48,128]{2,1,0:T(8,128)S(1)}, f32[16,48,128]{2,1,0:T(8,128)S(1)}, u32[]{:S(2)}, u32[]{:S(2)}) collective-permute-start(f32[16,48,128]{2,1,0:T(8,128)S(1)} %add.6.refs_2_), channel_id=1, source_target_pairs={{0,1},{1,0},{2,3},{3,2},{4,5},{5,4},{6,7},{7,6},{8,9},{9,8},{10,11... | collective-permute-start | bytes 1179656 | tf_op jit(solution)/shard_map/ppermute | solution.py:369
  123.7 14.0 %collective-permute-start.21 = (f32[16,48,128]{2,1,0:T(8,128)S(1)}, f32[16,48,128]{2,1,0:T(8,128)S(1)}, u32[]{:S(2)}, u32[]{:S(2)}) collective-permute-start(f32[16,48,128]{2,1,0:T(8,128)S(1)} %add.7.refs_3_), channel_id=1, source_target_pairs={{0,1},{1,0},{2,3},{3,2},{4,5},{5,4},{6,7},{7,6},{8,9},{9,8},{10,11... | collective-permute-start | bytes 1179656 | tf_op jit(solution)/shard_map/ppermute | solution.py:369

commit v3 on v2

--- a/solution.py
+++ b/solution.py
@@ -48,21 +48,54 @@
     return last, lax.rem(last + 127, 128)
 
 
-def ends_kernel(
-    velocity, x_first, x_last, y_first, y_last, z_first, z_last, uv, w_planes, w_rows, sems
-):
+def edges_kernel(velocity, x_first, x_last, y_first, y_last, tiles, sems):
+    _, X, rows, _ = velocity.shape
+    pieces = []
+    for k, comp in enumerate((0, 2)):
+        for i, at in enumerate((0, rows - 8)):
+            pieces.append((velocity.at[comp, :, at : at + 8, :], tiles.at[k, i]))
+    for k, comp in enumerate((1, 2)):
+        for out, at in ((x_first, 0), (x_last, X - 1)):
+            pieces.append((velocity.at[comp, at], out.at[k]))
+    copies = [pltpu.make_async_copy(a, b, sems.at[i]) for i, (a, b) in enumerate(pieces)]
+    for copy in copies:
+        copy.start()
+    for copy in copies[:4]:
+        copy.wait()
+    for k in range(2):
+        for p in range(X):
+            y_first[k, p : p + 1, :] = tiles[k, 0, p, 0:1, :]
+            y_last[k, p : p + 1, :] = tiles[k, 1, p, 7:8, :]
+    for copy in copies[4:]:
+        copy.wait()
+
+
+def edges(velocity):
+    _, X, Y, Z = velocity.shape
+    outs = [jax.ShapeDtypeStruct(s, F32) for s in ((2, Y, Z), (2, X, Z)) for _ in range(2)]
+    return pl.pallas_call(
+        edges_kernel,
+        in_specs=[pl.BlockSpec(memory_space=pl.ANY)],
+        out_specs=[pl.BlockSpec(memory_space=pltpu.VMEM)] * 4,
+        out_shape=outs,
+        scratch_shapes=[pltpu.VMEM((2, 2, X, 8, Z), F32), pltpu.SemaphoreType.DMA((8,))],
+        cost_estimate=pl.CostEstimate(flops=1_000_000, bytes_accessed=2_000_000, transcendentals=0),
+        name="edges",
+    )(velocity)
+
+
+def ends_kernel(velocity, z_first, z_last, uv, sems):
     _, X, rows, depth = velocity.shape
-    chunk = 4
-    chunks = X // chunk
-    pieces = [
-        (velocity.at[0:2, c * chunk : (c + 1) * chunk], uv.at[:, c * chunk : (c + 1) * chunk])
+    chunks = sems.shape[0]
+    chunk = X // chunks
+    copies = [
+        pltpu.make_async_copy(
+            velocity.at[0:2, c * chunk : (c + 1) * chunk],
+            uv.at[:, c * chunk : (c + 1) * chunk],
+            sems.at[c],
+        )
         for c in range(chunks)
     ]
-    pieces += [(velocity.at[2, at], w_planes.at[i]) for i, at in enumerate((0, X - 1))]
-    pieces += [
-        (velocity.at[2, :, at : at + 8, :], w_rows.at[i]) for i, at in enumerate((0, rows - 8))
-    ]
-    copies = [pltpu.make_async_copy(a, b, sems.at[i]) for i, (a, b) in enumerate(pieces)]
     for copy in copies:
         copy.start()
     lane = lax.broadcasted_iota(jnp.int32, (rows, 128), 1)
@@ -82,35 +115,19 @@
                     pltpu.roll(uv[k, p, :, depth - 128 :], (to_last + 1) % 128, 1),
                     last,
                 )
-            y_first[0, p : p + 1, :] = uv[0, p, 0:1, :]
-            y_last[0, p : p + 1, :] = uv[0, p, rows - 1 : rows, :]
     z_first[...] = first
     z_last[...] = last
-    for copy in copies[chunks:]:
-        copy.wait()
-    for i, (out, at) in enumerate(((x_first, 0), (x_last, X - 1))):
-        out[0] = uv[1, at]
-        out[1] = w_planes[i]
-    for p in range(X):
-        y_first[1, p : p + 1, :] = w_rows[0, p, 0:1, :]
-        y_last[1, p : p + 1, :] = w_rows[1, p, 7:8, :]
 
 
 def ends(velocity):
     _, X, Y, Z = velocity.shape
-    outs = [jax.ShapeDtypeStruct(s, F32) for s in ((2, Y, Z), (2, X, Z), (Y, 128)) for _ in range(2)]
     return pl.pallas_call(
         ends_kernel,
         in_specs=[pl.BlockSpec(memory_space=pl.ANY)],
-        out_specs=[pl.BlockSpec(memory_space=pltpu.VMEM)] * 6,
-        out_shape=outs,
-        scratch_shapes=[
-            pltpu.VMEM((2, X, Y, Z), F32),
-            pltpu.VMEM((2, Y, Z), F32),
-            pltpu.VMEM((2, X, 8, Z), F32),
-            pltpu.SemaphoreType.DMA((X // 4 + 4,)),
-        ],
-        cost_estimate=pl.CostEstimate(flops=4_000_000, bytes_accessed=8_000_000, transcendentals=0),
+        out_specs=[pl.BlockSpec(memory_space=pltpu.VMEM)] * 2,
+        out_shape=[jax.ShapeDtypeStruct((Y, 128), F32)] * 2,
+        scratch_shapes=[pltpu.VMEM((2, X, Y, Z), F32), pltpu.SemaphoreType.DMA((X // 4,))],
+        cost_estimate=pl.CostEstimate(flops=4_000_000, bytes_accessed=7_000_000, transcendentals=0),
         name="ends",
     )(velocity)
 
@@ -388,9 +405,10 @@
     at = lax.axis_index("gz").astype(jnp.int32)
     own = lax.shift_right_logical(at, jnp.int32(2))
     pos = jnp.stack([at, lax.shift_right_logical(at, jnp.int32(1)) ^ 2, 1 - own, own])
-    x_first, x_last, y_first, y_last, z_first, z_last = ends(velocity)
+    x_first, x_last, y_first, y_last = edges(velocity)
     y_halo = exchange(y_first, y_last, "gy")
     x_halo = exchange(x_first, x_last, "gx")
+    z_first, z_last = ends(velocity)
     z_halo = exchange(z_first, z_last, "gz")
     halos = (x_halo, y_halo, z_halo)
     blocks = {}

time: 141 us -> 142 us (level)
  the two profiles are of different devices: /device:TPU:57 before, /device:TPU:33 now
where the time goes in v3:
time: 142 us; the launch traced here: 141 us
  waiting for transfers between devices  63.2 us (45%)
  starting transfers between devices  39.2 us (28%)
  Pallas kernels  35 us (25%)
  other arithmetic  1.7 us (1%)
    ppermute x16, waiting for transfers between devices, send(): return lax.ppermute(value, 'gz', pairs)  58.9 us
    ppermute x16, starting transfers between devices, send(): return lax.ppermute(value, 'gz', pairs)  26 us
    pallas_call x3, Pallas kernels, curl(): pl.pallas_call(functools.partial(curl_kernel, shifts, each, with_level, w...  21.3 us
    ppermute x6, starting transfers between devices, exchange(): return (lax.ppermute(last, axis, up), lax.ppermute(first, axis, down))  13.2 us
    pallas_call x3, Pallas kernels, lay(): pl.pallas_call(functools.partial(lay_kernel, shifts), in_specs=in_specs,...  4.59 us
    ppermute x6, waiting for transfers between devices, exchange(): return (lax.ppermute(last, axis, up), lax.ppermute(first, axis, down))  4.34 us
    pallas_call x1, Pallas kernels, ends(): pl.pallas_call(ends_kernel, in_specs=[pl.BlockSpec(memory_space=pl.ANY)],...  3.99 us
    pallas_call x1, Pallas kernels, levels(): pl.pallas_call(levels_kernel, in_specs=[pl.BlockSpec(memory_space=pltpu.S...  3.02 us
  transfers between devices with their start and end apart: 22, of which 10 were waited for; matrix products, arithmetic and copies ran while one was open for 1% of the time, Pallas kernels for 10%

profile of v3, /device:TPU:33, one launch (start us, length us, event | category | flops | bytes accessed | tf_op | source)
XLA Modules:
  0.0 141.4 jit_solution(6080298473284264155)
XLA Ops:
  0.6 2.2 %edges.1 = (f32[2,96,256]{2,1,0:T(8,128)}, f32[2,96,256]{2,1,0:T(8,128)}, f32[2,32,256]{2,1,0:T(8,128)}, f32[2,32,256]{2,1,0:T(8,128)}) custom-call(f32[3,32,96,256]{3,2,1,0:T(8,128)} %refs_1_.5), custom_call_target="tpu_custom_call" | custom-call | flops 1000000 | bytes 2000000 | tf_op jit(solution)/shard_map/edges/pallas_call | solution.py:76
  2.8 1.3 collective-permute-start
  4.1 1.5 %collective-permute-start.1 = (f32[2,96,256]{2,1,0:T(8,128)}, f32[2,96,256]{2,1,0:T(8,128)S(1)}, u32[]{:S(2)}, u32[]{:S(2)}) collective-permute-start(f32[2,96,256]{2,1,0:T(8,128)} %get-tuple-element.28), channel_id=1, source_target_pairs={{64,0},{128,64},{192,128},{0,192},{65,1},{129,65},{193,129},{1,193... | collective-permute-start | bytes 589832 | tf_op jit(solution)/shard_map/ppermute | solution.py:401
  5.5 4.0 %ends.1 = (f32[96,128]{1,0:T(8,128)}, f32[96,128]{1,0:T(8,128)}) custom-call(f32[3,32,96,256]{3,2,1,0:T(8,128)} %refs_1_.5), custom_call_target="tpu_custom_call" | custom-call | flops 4000000 | bytes 7000000 | tf_op jit(solution)/shard_map/ends/pallas_call | solution.py:124
  9.5 2.8 %collective-permute-start.4 = (f32[96,128]{1,0:T(8,128)}, f32[96,128]{1,0:T(8,128)S(1)}, u32[]{:S(2)}, u32[]{:S(2)}) collective-permute-start(f32[96,128]{1,0:T(8,128)} %get-tuple-element.31), channel_id=1, source_target_pairs={{0,1},{1,2},{2,3},{3,4},{4,5},{5,6},{6,7},{7,0},{8,9},{9,10},{10,1... | collective-permute-start | bytes 147464 | tf_op jit(solution)/shard_map/ppermute | solution.py:401
  12.4 0.0 copy-done.10
  12.4 1.3 collective-permute-start.2
  13.7 0.0 copy-done.9
  13.7 6.3 %collective-permute-start.3 = (f32[2,32,256]{2,1,0:T(8,128)S(1)}, f32[2,32,256]{2,1,0:T(8,128)S(1)}, u32[]{:S(2)}, u32[]{:S(2)}) collective-permute-start(f32[2,32,256]{2,1,0:T(8,128)S(1)} %copy-done.9), channel_id=1, source_target_pairs={{8,0},{16,8},{24,16},{32,24},{40,32},{48,40},{56,48},{0,56},{9,1},... | collective-permute-start | bytes 196616 | tf_op jit(solution)/shard_map/ppermute | solution.py:401
  20.0 0.0 collective-permute-done.4.refs_6_
  20.0 0.0 collective-permute-start.5
  20.0 0.6 pad_add_fusion.pos
  20.7 4.3 %collective-permute-done.5.refs_7_ = f32[96,128]{1,0:T(8,128)S(1)} collective-permute-done((f32[96,128]{1,0:T(8,128)}, f32[96,128]{1,0:T(8,128)S(1)}, u32[]{:S(2)}, u32[]{:S(2)}) %collective-permute-start.5) | collective-permute-done | bytes 49184 | tf_op jit(solution)/shard_map/ppermute | solution.py:401
  25.0 0.0 collective-permute-done.2.refs_4_
  25.0 0.0 collective-permute-done.3.refs_5_
  25.0 0.0 copy-start.6
  25.0 0.0 collective-permute-done.refs_2_
  25.0 0.0 copy-start.3
  25.0 0.0 collective-permute-done.1.refs_3_
  25.0 0.6 copy-done.8
  25.6 0.0 copy-done.5
  25.6 0.0 copy-done.6
  25.6 0.1 copy-done.3
  25.7 0.7 copy-done.4
  26.4 7.8 %curl.3 = (f32[12,32,256]{2,1,0:T(8,128)}, f32[12,32,256]{2,1,0:T(8,128)}, f32[16,48,128]{2,1,0:T(8,128)}) custom-call(s32[4]{0:T(128)} %pad_add_fusion.pos, f32[3,32,96,256]{3,2,1,0:T(8,128)} %refs_1_.5, f32[3,32,96,256]{3,2,1,0:T(8,128)} %refs_1_.5, f32[3,32,96,256]{3,2,1,0:T(8,128)} %refs_1_.5, f32[3,32,96,256]{3,2,1,0:T(8,128)} %refs_1_.5, ...), custom_call_target="tpu_custom_call" | custom-call | flops 7864320 | bytes 7864320 | tf_op jit(solution)/shard_map/curl/pallas_call | solution.py:277
  34.2 7.9 %curl.4 = (f32[12,32,256]{2,1,0:T(8,128)}, f32[12,32,256]{2,1,0:T(8,128)}, f32[12,32,256]{2,1,0:T(8,128)}, f32[12,32,256]{2,1,0:T(8,128)}, f32[16,48,128]{2,1,0:T(8,128)}) custom-call(s32[4]{0:T(128)} %pad_add_fusion.pos, f32[3,32,96,256]{3,2,1,0:T(8,128)} %refs_1_.5, f32[3,32,96,256]{3,2,1,0:T(8,128)} %refs_1_.5, ...), custom_call_target="tpu_custom_call", output_to_operand_aliasing={{4}: (14, {})} | custom-call | flops 7864320 | bytes 7864320 | tf_op jit(solution)/shard_map/curl/pallas_call | solution.py:277
  42.1 1.0 collective-permute-start.13
  43.1 3.9 %collective-permute-start.14 = (f32[16,48,128]{2,1,0:T(8,128)}, f32[16,48,128]{2,1,0:T(8,128)S(1)}, u32[]{:S(2)}, u32[]{:S(2)}) collective-permute-start(f32[16,48,128]{2,1,0:T(8,128)} %get-tuple-element.42.refs_0_), channel_id=1, source_target_pairs={{2,4},{3,5},{4,2},{5,3},{10,12},{11,13},{12,10},{13,11},{18,20},{1... | collective-permute-start | bytes 1179656 | tf_op jit(solution)/shard_map/ppermute | solution.py:386
  47.0 6.0 %collective-permute-done.13.refs_1_ = f32[16,48,128]{2,1,0:T(8,128)S(1)} collective-permute-done((f32[16,48,128]{2,1,0:T(8,128)}, f32[16,48,128]{2,1,0:T(8,128)S(1)}, u32[]{:S(2)}, u32[]{:S(2)}) %collective-permute-start.13) | collective-permute-done | bytes 393248 | tf_op jit(solution)/shard_map/ppermute | solution.py:386
  53.0 3.0 %collective-permute-start.16 = (f32[16,48,128]{2,1,0:T(8,128)S(1)}, f32[16,48,128]{2,1,0:T(8,128)S(1)}, u32[]{:S(2)}, u32[]{:S(2)}) collective-permute-start(f32[16,48,128]{2,1,0:T(8,128)S(1)} %collective-permute-done.13.refs_1_), channel_id=1, source_target_pairs={{2,4},{3,5},{4,2},{5,3},{10,12},{11,13},{12,10},{13,11},{18,20},{1... | collective-permute-start | bytes 1179656 | tf_op jit(solution)/shard_map/ppermute | solution.py:386
  56.0 0.1 collective-permute-start.7
  56.1 0.8 collective-permute-done.14
  56.8 2.6 %collective-permute-start.15 = (f32[16,48,128]{2,1,0:T(8,128)S(1)}, f32[16,48,128]{2,1,0:T(8,128)S(1)}, u32[]{:S(2)}, u32[]{:S(2)}) collective-permute-start(f32[16,48,128]{2,1,0:T(8,128)S(1)} %collective-permute-done.14), channel_id=1, source_target_pairs={{2,0},{3,1},{4,6},{5,7},{10,8},{11,9},{12,14},{13,15},{18,16},{19,... | collective-permute-start | bytes 1179656 | tf_op jit(solution)/shard_map/ppermute | solution.py:386
  59.4 6.2 %collective-permute-done.16 = f32[16,48,128]{2,1,0:T(8,128)S(1)} collective-permute-done((f32[16,48,128]{2,1,0:T(8,128)S(1)}, f32[16,48,128]{2,1,0:T(8,128)S(1)}, u32[]{:S(2)}, u32[]{:S(2)}) %collective-permute-start.16) | collective-permute-done | bytes 393248 | tf_op jit(solution)/shard_map/ppermute | solution.py:386
  65.7 2.0 %collective-permute-start.17 = (f32[16,48,128]{2,1,0:T(8,128)S(1)}, f32[16,48,128]{2,1,0:T(8,128)}, u32[]{:S(2)}, u32[]{:S(2)}) collective-permute-start(f32[16,48,128]{2,1,0:T(8,128)S(1)} %collective-permute-done.16), channel_id=1, source_target_pairs={{2,0},{3,1},{4,6},{5,7},{10,8},{11,9},{12,14},{13,15},{18,16},{19,... | collective-permute-start | bytes 1179656 | tf_op jit(solution)/shard_map/ppermute | solution.py:386
  67.7 1.3 collective-permute-start.8
  69.0 0.6 collective-permute-start.9
  69.6 5.6 %curl.5 = (f32[12,32,256]{2,1,0:T(8,128)}, f32[12,32,256]{2,1,0:T(8,128)}) custom-call(s32[4]{0:T(128)} %pad_add_fusion.pos, f32[3,32,96,256]{3,2,1,0:T(8,128)} %refs_1_.5, f32[3,32,96,256]{3,2,1,0:T(8,128)} %refs_1_.5, f32[3,32,96,256]{3,2,1,0:T(8,128)} %refs_1_.5, f32[3,32,96,256]{3,2,1,0:T(8,128)} %refs_1_.5, f32[3,32,96,256]{3,2,1,0:T(8,128)} %refs_1_.5, ...), custom_call_target="tpu_custom_call" | custom-call | flops 3932160 | bytes 3932160 | tf_op jit(solution)/shard_map/curl/pallas_call | solution.py:277
  75.2 0.0 collective-permute-done.7.refs_0_
  75.2 0.1 collective-permute-start.10
  75.3 6.7 %collective-permute-done.15 = f32[16,48,128]{2,1,0:T(8,128)S(1)} collective-permute-done((f32[16,48,128]{2,1,0:T(8,128)S(1)}, f32[16,48,128]{2,1,0:T(8,128)S(1)}, u32[]{:S(2)}, u32[]{:S(2)}) %collective-permute-start.15) | collective-permute-done | bytes 393248 | tf_op jit(solution)/shard_map/ppermute | solution.py:386
  82.0 2.0 %collective-permute-start.11 = (f32[12,32,256]{2,1,0:T(8,128)}, f32[12,32,256]{2,1,0:T(8,128)S(1)}, u32[]{:S(2)}, u32[]{:S(2)}) collective-permute-start(f32[12,32,256]{2,1,0:T(8,128)} %get-tuple-element.40), channel_id=1, source_target_pairs={{0,4},{1,5},{2,6},{3,7},{4,0},{5,1},{6,2},{7,3},{8,12},{9,13},{10,... | collective-permute-start | bytes 1179656 | tf_op jit(solution)/shard_map/ppermute | solution.py:386
  84.0 6.8 %collective-permute-done.17 = f32[16,48,128]{2,1,0:T(8,128)} collective-permute-done((f32[16,48,128]{2,1,0:T(8,128)S(1)}, f32[16,48,128]{2,1,0:T(8,128)}, u32[]{:S(2)}, u32[]{:S(2)}) %collective-permute-start.17) | collective-permute-done | bytes 393248 | tf_op jit(solution)/shard_map/ppermute | solution.py:386
  90.8 3.7 %collective-permute-start.12 = (f32[12,32,256]{2,1,0:T(8,128)}, f32[12,32,256]{2,1,0:T(8,128)S(1)}, u32[]{:S(2)}, u32[]{:S(2)}) collective-permute-start(f32[12,32,256]{2,1,0:T(8,128)} %get-tuple-element.41), channel_id=1, source_target_pairs={{0,5},{1,4},{2,7},{3,6},{4,1},{5,0},{6,3},{7,2},{8,13},{9,12},{10,... | collective-permute-start | bytes 1179656 | tf_op jit(solution)/shard_map/ppermute | solution.py:386
  94.6 1.1 add.7.refs_3_
  95.7 0.0 collective-permute-done.8.refs_1_
  95.7 0.1 collective-permute-start.18
  95.8 0.0 collective-permute-done.9.refs_1_
  95.8 0.4 collective-permute-start.6
  96.2 3.2 %collective-permute-done.10.refs_2_ = f32[12,32,256]{2,1,0:T(8,128)S(1)} collective-permute-done((f32[12,32,256]{2,1,0:T(8,128)}, f32[12,32,256]{2,1,0:T(8,128)S(1)}, u32[]{:S(2)}, u32[]{:S(2)}) %collective-permute-start.10) | collective-permute-done | bytes 393248 | tf_op jit(solution)/shard_map/ppermute | solution.py:386
  99.4 0.4 collective-permute-start.19
  99.8 17.8 %collective-permute-done.11.refs_3_ = f32[12,32,256]{2,1,0:T(8,128)S(1)} collective-permute-done((f32[12,32,256]{2,1,0:T(8,128)}, f32[12,32,256]{2,1,0:T(8,128)S(1)}, u32[]{:S(2)}, u32[]{:S(2)}) %collective-permute-start.11) | collective-permute-done | bytes 393248 | tf_op jit(solution)/shard_map/ppermute | solution.py:386
  117.6 2.4 %collective-permute-start.20 = (f32[16,48,128]{2,1,0:T(8,128)S(1)}, f32[16,48,128]{2,1,0:T(8,128)S(1)}, u32[]{:S(2)}, u32[]{:S(2)}) collective-permute-start(f32[16,48,128]{2,1,0:T(8,128)S(1)} %add.6.refs_2_), channel_id=1, source_target_pairs={{0,1},{1,0},{2,3},{3,2},{4,5},{5,4},{6,7},{7,6},{8,9},{9,8},{10,11... | collective-permute-start | bytes 1179656 | tf_op jit(solution)/shard_map/ppermute | solution.py:386
  119.9 6.0 %collective-permute-done.12.refs_4_ = f32[12,32,256]{2,1,0:T(8,128)S(1)} collective-permute-done((f32[12,32,256]{2,1,0:T(8,128)}, f32[12,32,256]{2,1,0:T(8,128)S(1)}, u32[]{:S(2)}, u32[]{:S(2)}) %collective-permute-start.12) | collective-permute-done | bytes 393248 | tf_op jit(solution)/shard_map/ppermute | solution.py:386
  126.0 2.4 %collective-permute-start.21 = (f32[16,48,128]{2,1,0:T(8,128)S(1)}, f32[16,48,128]{2,1,0:T(8,128)S(1)}, u32[]{:S(2)}, u32[]{:S(2)}) collective-permute-start(f32[16,48,128]{2,1,0:T(8,128)S(1)} %add.7.refs_3_), channel_id=1, source_target_pairs={{0,1},{1,0},{2,3},{3,2},{4,5},{5,4},{6,7},{7,6},{8,9},{9,8},{10,11... | collective-permute-start | bytes 1179656 | tf_op jit(solution)/shard_map/ppermute | solution.py:386
  128.4 1.8 %lay.3.refs_2_ = f32[12,32,2048]{2,1,0:T(8,128)} custom-call(s32[4]{0:T(128)S(1)} %copy-done.2, f32[12,32,256]{2,1,0:T(8,128)S(1)} %copy-done.1, f32[12,32,256]{2,1,0:T(8,128)S(1)} %collective-permute-done.9.refs_1_, f32[12,32,256]{2,1,0:T(8,128)S(1)} %collective-permute-done.10.refs_2_, f32[12,32,256]{2,1,0:T(8,128)S(1)} %collective-permute-done.11.refs_3_, ...), custom_call_target="tpu_custom_call" | custom-call | flops 491520 | bytes 3932160 | tf_op jit(solution)/shard_map/lay/pallas_call | solution.py:320
  130.2 1.4 %lay.4.refs_1_ = f32[12,32,2048]{2,1,0:T(8,128)} custom-call(s32[4]{0:T(128)S(1)} %copy-done.2, f32[12,32,256]{2,1,0:T(8,128)S(1)} %collective-permute-done.7.refs_0_, f32[12,32,256]{2,1,0:T(8,128)S(1)} %collective-permute-done.8.refs_1_, f32[12,32,2048]{2,1,0:T(8,128)} %lay.3.refs_2_), custom_call_target="tpu_custom_call", output_to_operand_aliasing={{}: (3, {})} | custom-call | flops 196608 | bytes 1572864 | tf_op jit(solution)/shard_map/lay/pallas_call | solution.py:320
  131.7 5.3 %collective-permute-done.6.refs_0_ = f32[12,32,256]{2,1,0:T(8,128)S(1)} collective-permute-done((f32[12,32,256]{2,1,0:T(8,128)}, f32[12,32,256]{2,1,0:T(8,128)S(1)}, u32[]{:S(2)}, u32[]{:S(2)}) %collective-permute-start.6) | collective-permute-done | bytes 393248 | tf_op jit(solution)/shard_map/ppermute | solution.py:386
  137.0 1.3 lay.5
  138.3 0.0 collective-permute-done.18.refs_4_
  138.3 0.0 collective-permute-done.19.refs_5_
  138.3 0.0 collective-permute-done.20.refs_6_
  138.3 0.0 collective-permute-done.21.refs_7_
  138.3 3.0 %levels.1 = (f32[16,48,1024]{2,1,0:T(8,128)}, f32[8,24,512]{2,1,0:T(8,128)}, f32[12,4,256]{2,1,0:T(4,128)}, f32[6,2,128]{2,1,0:T(2,128)}, f32[3,1,64]{2,1,0:T(1,128)}) custom-call(s32[4]{0:T(128)S(1)} %copy-done.2, f32[16,48,128]{2,1,0:T(8,128)S(1)} %copy-done, f32[16,48,128]{2,1,0:T(8,128)S(1)} %collective-permute-done.13.refs_1_, ...), custom_call_target="tpu_custom_call" | custom-call | flops 3145728 | bytes 7864320 | tf_op jit(solution)/shard_map/levels/pallas_call | solution.py:371
  (14 shorter events, 0.1 us)
Async XLA Ops:
  2.8 22.2 %collective-permute-start = (f32[2,96,256]{2,1,0:T(8,128)}, f32[2,96,256]{2,1,0:T(8,128)S(1)}, u32[]{:S(2)}, u32[]{:S(2)}) collective-permute-start(f32[2,96,256]{2,1,0:T(8,128)} %get-tuple-element.27), channel_id=1, source_target_pairs={{0,64},{64,128},{128,192},{192,0},{1,65},{65,129},{129,193},{193,1... | collective-permute-start | bytes 589832 | tf_op jit(solution)/shard_map/ppermute | solution.py:401
  4.1 8.3 %copy-start.10 = (f32[2,32,256]{2,1,0:T(8,128)S(1)}, f32[2,32,256]{2,1,0:T(8,128)}, u32[]{:S(2)}) copy-start(f32[2,32,256]{2,1,0:T(8,128)} %get-tuple-element.29) | copy-start | bytes 196612
  4.1 9.6 %copy-start.9 = (f32[2,32,256]{2,1,0:T(8,128)S(1)}, f32[2,32,256]{2,1,0:T(8,128)}, u32[]{:S(2)}) copy-start(f32[2,32,256]{2,1,0:T(8,128)} %get-tuple-element.30) | copy-start | bytes 196612
  4.1 20.9 %collective-permute-start.1 = (f32[2,96,256]{2,1,0:T(8,128)}, f32[2,96,256]{2,1,0:T(8,128)S(1)}, u32[]{:S(2)}, u32[]{:S(2)}) collective-permute-start(f32[2,96,256]{2,1,0:T(8,128)} %get-tuple-element.28), channel_id=1, source_target_pairs={{64,0},{128,64},{192,128},{0,192},{65,1},{129,65},{193,129},{1,193... | collective-permute-start | bytes 589832 | tf_op jit(solution)/shard_map/ppermute | solution.py:401
  9.5 10.5 %collective-permute-start.4 = (f32[96,128]{1,0:T(8,128)}, f32[96,128]{1,0:T(8,128)S(1)}, u32[]{:S(2)}, u32[]{:S(2)}) collective-permute-start(f32[96,128]{1,0:T(8,128)} %get-tuple-element.31), channel_id=1, source_target_pairs={{0,1},{1,2},{2,3},{3,4},{4,5},{5,6},{6,7},{7,0},{8,9},{9,10},{10,1... | collective-permute-start | bytes 147464 | tf_op jit(solution)/shard_map/ppermute | solution.py:401
  12.4 12.6 %collective-permute-start.2 = (f32[2,32,256]{2,1,0:T(8,128)S(1)}, f32[2,32,256]{2,1,0:T(8,128)S(1)}, u32[]{:S(2)}, u32[]{:S(2)}) collective-permute-start(f32[2,32,256]{2,1,0:T(8,128)S(1)} %copy-done.10), channel_id=1, source_target_pairs={{0,8},{8,16},{16,24},{24,32},{32,40},{40,48},{48,56},{56,0},{1,9},... | collective-permute-start | bytes 196616 | tf_op jit(solution)/shard_map/ppermute | solution.py:401
  13.7 11.3 %collective-permute-start.3 = (f32[2,32,256]{2,1,0:T(8,128)S(1)}, f32[2,32,256]{2,1,0:T(8,128)S(1)}, u32[]{:S(2)}, u32[]{:S(2)}) collective-permute-start(f32[2,32,256]{2,1,0:T(8,128)S(1)} %copy-done.9), channel_id=1, source_target_pairs={{8,0},{16,8},{24,16},{32,24},{40,32},{48,40},{56,48},{0,56},{9,1},... | collective-permute-start | bytes 196616 | tf_op jit(solution)/shard_map/ppermute | solution.py:401
  20.0 5.0 %copy-start.7 = (f32[96,128]{1,0:T(8,128)}, f32[96,128]{1,0:T(8,128)S(1)}, u32[]{:S(2)}) copy-start(f32[96,128]{1,0:T(8,128)S(1)} %collective-permute-done.4.refs_6_) | copy-start | bytes 147460
  20.0 4.9 %collective-permute-start.5 = (f32[96,128]{1,0:T(8,128)}, f32[96,128]{1,0:T(8,128)S(1)}, u32[]{:S(2)}, u32[]{:S(2)}) collective-permute-start(f32[96,128]{1,0:T(8,128)} %get-tuple-element.32), channel_id=1, source_target_pairs={{1,0},{2,1},{3,2},{4,3},{5,4},{6,5},{7,6},{0,7},{9,8},{10,9},{11,1... | collective-permute-start | bytes 147464 | tf_op jit(solution)/shard_map/ppermute | solution.py:401
  25.0 0.6 copy-start.8
  25.0 0.6 copy-start.5
  25.0 0.6 copy-start.6
  25.0 0.7 copy-start.3
  25.7 0.7 copy-start.4
  42.1 10.9 %collective-permute-start.13 = (f32[16,48,128]{2,1,0:T(8,128)}, f32[16,48,128]{2,1,0:T(8,128)S(1)}, u32[]{:S(2)}, u32[]{:S(2)}) collective-permute-start(f32[16,48,128]{2,1,0:T(8,128)} %get-tuple-element.42.refs_0_), channel_id=1, source_target_pairs={{0,2},{1,3},{2,0},{3,1},{4,6},{5,7},{6,4},{7,5},{8,10},{9,11},{10,... | collective-permute-start | bytes 1179656 | tf_op jit(solution)/shard_map/ppermute | solution.py:386
  43.1 13.8 %collective-permute-start.14 = (f32[16,48,128]{2,1,0:T(8,128)}, f32[16,48,128]{2,1,0:T(8,128)S(1)}, u32[]{:S(2)}, u32[]{:S(2)}) collective-permute-start(f32[16,48,128]{2,1,0:T(8,128)} %get-tuple-element.42.refs_0_), channel_id=1, source_target_pairs={{2,4},{3,5},{4,2},{5,3},{10,12},{11,13},{12,10},{13,11},{18,20},{1... | collective-permute-start | bytes 1179656 | tf_op jit(solution)/shard_map/ppermute | solution.py:386
  53.0 12.7 %collective-permute-start.16 = (f32[16,48,128]{2,1,0:T(8,128)S(1)}, f32[16,48,128]{2,1,0:T(8,128)S(1)}, u32[]{:S(2)}, u32[]{:S(2)}) collective-permute-start(f32[16,48,128]{2,1,0:T(8,128)S(1)} %collective-permute-done.13.refs_1_), channel_id=1, source_target_pairs={{2,4},{3,5},{4,2},{5,3},{10,12},{11,13},{12,10},{13,11},{18,20},{1... | collective-permute-start | bytes 1179656 | tf_op jit(solution)/shard_map/ppermute | solution.py:386
  56.0 19.3 %collective-permute-start.7 = (f32[12,32,256]{2,1,0:T(8,128)}, f32[12,32,256]{2,1,0:T(8,128)S(1)}, u32[]{:S(2)}, u32[]{:S(2)}) collective-permute-start(f32[12,32,256]{2,1,0:T(8,128)} %get-tuple-element.35), channel_id=1, source_target_pairs={{0,2},{1,3},{2,0},{3,1},{4,6},{5,7},{6,4},{7,5},{8,10},{9,11},{10,... | collective-permute-start | bytes 1179656 | tf_op jit(solution)/shard_map/ppermute | solution.py:386
  56.8 25.2 %collective-permute-start.15 = (f32[16,48,128]{2,1,0:T(8,128)S(1)}, f32[16,48,128]{2,1,0:T(8,128)S(1)}, u32[]{:S(2)}, u32[]{:S(2)}) collective-permute-start(f32[16,48,128]{2,1,0:T(8,128)S(1)} %collective-permute-done.14), channel_id=1, source_target_pairs={{2,0},{3,1},{4,6},{5,7},{10,8},{11,9},{12,14},{13,15},{18,16},{19,... | collective-permute-start | bytes 1179656 | tf_op jit(solution)/shard_map/ppermute | solution.py:386
  65.7 25.2 %collective-permute-start.17 = (f32[16,48,128]{2,1,0:T(8,128)S(1)}, f32[16,48,128]{2,1,0:T(8,128)}, u32[]{:S(2)}, u32[]{:S(2)}) collective-permute-start(f32[16,48,128]{2,1,0:T(8,128)S(1)} %collective-permute-done.16), channel_id=1, source_target_pairs={{2,0},{3,1},{4,6},{5,7},{10,8},{11,9},{12,14},{13,15},{18,16},{19,... | collective-permute-start | bytes 1179656 | tf_op jit(solution)/shard_map/ppermute | solution.py:386
  67.7 28.0 %collective-permute-start.8 = (f32[12,32,256]{2,1,0:T(8,128)}, f32[12,32,256]{2,1,0:T(8,128)S(1)}, u32[]{:S(2)}, u32[]{:S(2)}) collective-permute-start(f32[12,32,256]{2,1,0:T(8,128)} %get-tuple-element.36), channel_id=1, source_target_pairs={{0,6},{1,7},{2,4},{3,5},{4,2},{5,3},{6,0},{7,1},{8,14},{9,15},{10,... | collective-permute-start | bytes 1179656 | tf_op jit(solution)/shard_map/ppermute | solution.py:386
  69.0 26.6 %copy-start = (f32[16,48,128]{2,1,0:T(8,128)S(1)}, f32[16,48,128]{2,1,0:T(8,128)}, u32[]{:S(2)}) copy-start(f32[16,48,128]{2,1,0:T(8,128)} %get-tuple-element.42.refs_0_) | copy-start | bytes 1179652
  69.0 59.3 %copy-start.1 = (f32[12,32,256]{2,1,0:T(8,128)S(1)}, f32[12,32,256]{2,1,0:T(8,128)}, u32[]{:S(2)}) copy-start(f32[12,32,256]{2,1,0:T(8,128)} %get-tuple-element.37.refs_0_) | copy-start | bytes 1179652
  69.0 59.3 %copy-start.2 = (s32[4]{0:T(128)S(1)}, s32[4]{0:T(128)}, u32[]{:S(2)}) copy-start(s32[4]{0:T(128)} %pad_add_fusion.pos) | copy-start | bytes 52
  69.0 26.7 %collective-permute-start.9 = (f32[12,32,256]{2,1,0:T(8,128)}, f32[12,32,256]{2,1,0:T(8,128)S(1)}, u32[]{:S(2)}, u32[]{:S(2)}) collective-permute-start(f32[12,32,256]{2,1,0:T(8,128)} %get-tuple-element.38), channel_id=1, source_target_pairs={{0,1},{1,0},{2,3},{3,2},{4,5},{5,4},{6,7},{7,6},{8,9},{9,8},{10,11... | collective-permute-start | bytes 1179656 | tf_op jit(solution)/shard_map/ppermute | solution.py:386
  75.2 24.1 %collective-permute-start.10 = (f32[12,32,256]{2,1,0:T(8,128)}, f32[12,32,256]{2,1,0:T(8,128)S(1)}, u32[]{:S(2)}, u32[]{:S(2)}) collective-permute-start(f32[12,32,256]{2,1,0:T(8,128)} %get-tuple-element.39), channel_id=1, source_target_pairs={{0,3},{1,2},{2,1},{3,0},{4,7},{5,6},{6,5},{7,4},{8,11},{9,10},{10,... | collective-permute-start | bytes 1179656 | tf_op jit(solution)/shard_map/ppermute | solution.py:386
  82.0 35.5 %collective-permute-start.11 = (f32[12,32,256]{2,1,0:T(8,128)}, f32[12,32,256]{2,1,0:T(8,128)S(1)}, u32[]{:S(2)}, u32[]{:S(2)}) collective-permute-start(f32[12,32,256]{2,1,0:T(8,128)} %get-tuple-element.40), channel_id=1, source_target_pairs={{0,4},{1,5},{2,6},{3,7},{4,0},{5,1},{6,2},{7,3},{8,12},{9,13},{10,... | collective-permute-start | bytes 1179656 | tf_op jit(solution)/shard_map/ppermute | solution.py:386
  90.8 35.1 %collective-permute-start.12 = (f32[12,32,256]{2,1,0:T(8,128)}, f32[12,32,256]{2,1,0:T(8,128)S(1)}, u32[]{:S(2)}, u32[]{:S(2)}) collective-permute-start(f32[12,32,256]{2,1,0:T(8,128)} %get-tuple-element.41), channel_id=1, source_target_pairs={{0,5},{1,4},{2,7},{3,6},{4,1},{5,0},{6,3},{7,2},{8,13},{9,12},{10,... | collective-permute-start | bytes 1179656 | tf_op jit(solution)/shard_map/ppermute | solution.py:386
  95.7 42.6 %collective-permute-start.18 = (f32[16,48,128]{2,1,0:T(8,128)S(1)}, f32[16,48,128]{2,1,0:T(8,128)S(1)}, u32[]{:S(2)}, u32[]{:S(2)}) collective-permute-start(f32[16,48,128]{2,1,0:T(8,128)S(1)} %copy-done), channel_id=1, source_target_pairs={{0,1},{1,0},{2,3},{3,2},{4,5},{5,4},{6,7},{7,6},{8,9},{9,8},{10,11... | collective-permute-start | bytes 1179656 | tf_op jit(solution)/shard_map/ppermute | solution.py:386
  95.8 41.2 %collective-permute-start.6 = (f32[12,32,256]{2,1,0:T(8,128)}, f32[12,32,256]{2,1,0:T(8,128)S(1)}, u32[]{:S(2)}, u32[]{:S(2)}) collective-permute-start(f32[12,32,256]{2,1,0:T(8,128)} %get-tuple-element.33), channel_id=1, source_target_pairs={{0,7},{1,6},{2,5},{3,4},{4,3},{5,2},{6,1},{7,0},{8,15},{9,14},{10,... | collective-permute-start | bytes 1179656 | tf_op jit(solution)/shard_map/ppermute | solution.py:386
  99.4 38.9 %collective-permute-start.19 = (f32[16,48,128]{2,1,0:T(8,128)S(1)}, f32[16,48,128]{2,1,0:T(8,128)S(1)}, u32[]{:S(2)}, u32[]{:S(2)}) collective-permute-start(f32[16,48,128]{2,1,0:T(8,128)S(1)} %collective-permute-done.13.refs_1_), channel_id=1, source_target_pairs={{0,1},{1,0},{2,3},{3,2},{4,5},{5,4},{6,7},{7,6},{8,9},{9,8},{10,11... | collective-permute-start | bytes 1179656 | tf_op jit(solution)/shard_map/ppermute | solution.py:386
  117.6 20.8 %collective-permute-start.20 = (f32[16,48,128]{2,1,0:T(8,128)S(1)}, f32[16,48,128]{2,1,0:T(8,128)S(1)}, u32[]{:S(2)}, u32[]{:S(2)}) collective-permute-start(f32[16,48,128]{2,1,0:T(8,128)S(1)} %add.6.refs_2_), channel_id=1, source_target_pairs={{0,1},{1,0},{2,3},{3,2},{4,5},{5,4},{6,7},{7,6},{8,9},{9,8},{10,11... | collective-permute-start | bytes 1179656 | tf_op jit(solution)/shard_map/ppermute | solution.py:386
  126.0 12.3 %collective-permute-start.21 = (f32[16,48,128]{2,1,0:T(8,128)S(1)}, f32[16,48,128]{2,1,0:T(8,128)S(1)}, u32[]{:S(2)}, u32[]{:S(2)}) collective-permute-start(f32[16,48,128]{2,1,0:T(8,128)S(1)} %add.7.refs_3_), channel_id=1, source_target_pairs={{0,1},{1,0},{2,3},{3,2},{4,5},{5,4},{6,7},{7,6},{8,9},{9,8},{10,11... | collective-permute-start | bytes 1179656 | tf_op jit(solution)/shard_map/ppermute | solution.py:386
